TPU v7x, 32 devices: a whole 2x2x4 slice. The times are simulated.
32 devices in a mesh: dp: 8 (over y, x, core), tensor: 4 (over z).
Axes of the slice: x: 2, y: 2, z: 4, core: 2. Of those that a mesh axis runs over, the one named last changes fastest.
Arguments:
- text: bfloat16 [8, 256, 5120], P('dp', None, 'tensor'), may hold values from -6 to 6
- prompts: bfloat16 [8, 100, 5120], P('dp', None, 'tensor'), may hold values from -6 to 6
- gain: float32 [5120], replicated, may hold values from 0.1 to 1.9
- w_query: bfloat16 [5120, 3072], P(None, 'tensor'), may hold values from -0.069877124 to 0.069877124, as said below
- w_key: bfloat16 [5120, 3072], P(None, 'tensor'), may hold values from -1.2577882 to 1.2577882, as said below
- w_value: bfloat16 [5120, 3072], P(None, 'tensor'), may hold values from -0.078125 to 0.078125
- cotangent: bfloat16 [8, 356, 3072], P('dp', None, 'tensor'), may hold values from -6 to 6
- task_of: int32 [8], replicated, may hold values from 0 to 7, as said below
- lengths: int32 [8], replicated, may hold values from 1 to 256, as said below
- slot: int32 [8], replicated, may hold values from 0 to 7, as said below
Outputs:
- attn_out: bfloat16 [8, 356, 3072], P('dp', None, 'tensor')
- prompt_grad: float32 [8, 100, 5120], P('dp', None, 'tensor')
Inputs may be any that keep to these rules, and one draw needn't show every extreme that they name: `task_of`: nondecreasing along the source order. `lengths`: some example has exactly 256 text tokens; rows of an example beyond its length are padding. `slot`: a permutation of 0 to 7; position s lies on index s // 1 of dp. `w_query`: entries of order 5120 ** -0.5. `w_key`: entries of order 5120 ** -0.5 or larger.
All inputs are finite; a program needn't handle non-finite values.
Results may differ from a plain program's by a relative error of at most 0.0082.
Values may be sent and summed in bfloat16 or wider, within the bound.
No kernel may reach another device: no remote copies, remote signals or barrier semaphores. Data moves between devices by JAX's collectives and lax.ppermute only.
A program may use at most 128 MiB of HBM per device.

v0:
```python
import functools
import math

import jax
import jax.numpy as jnp
from jax import lax
from jax.experimental import pallas as pl
from jax.experimental.pallas import tpu as pltpu
from jax.sharding import PartitionSpec as P


HD = 128
BF16, F32 = jnp.bfloat16, jnp.float32
VM = pl.BlockSpec(memory_space=pltpu.VMEM)
SM = pl.BlockSpec(memory_space=pltpu.SMEM)
ANY = pl.BlockSpec(memory_space=pl.ANY)
PAIR = 2
LIMIT = 16 << 20
WAIT = 10**9


def up_to(value, step):
    return -(-value // step) * step


def call(body, outs, in_specs, args, scratch=(), flops=WAIT, limit=LIMIT):
    return pl.pallas_call(
        body,
        out_shape=[jax.ShapeDtypeStruct(s, d) for s, d in outs],
        in_specs=in_specs,
        out_specs=[VM] * len(outs),
        scratch_shapes=list(scratch),
        cost_estimate=pl.CostEstimate(flops=flops, bytes_accessed=1 << 20, transcendentals=0),
        compiler_params=pltpu.CompilerParams(vmem_limit_bytes=limit),
    )(*args)


def partner(me, k, count):
    return me ^ k if count & (count - 1) == 0 else lax.rem(me + k, count)


def group_pairs(count, k):
    pairs = []
    for g in range(count):
        to = g ^ k if count & (count - 1) == 0 else (g + k) % count
        pairs += [(g * PAIR + c, to * PAIR + c) for c in range(PAIR)]
    return pairs


def came_from(me, k, count):
    return me ^ k if count & (count - 1) == 0 else lax.rem(me + count - k, count)


def step_of(source, me, count):
    return source ^ me if count & (count - 1) == 0 else lax.rem(me + count - source, count)


def far_first(count):
    return sorted(range(1, count), key=lambda k: -bin(k).count("1"))


def to_groups(blocks):
    count = len(blocks)
    got = [blocks[0]] + [None] * (count - 1)
    for k in far_first(count):
        got[k] = lax.ppermute(blocks[k], "dp", group_pairs(count, k))
    return got


def to_sibling(block):
    count = lax.axis_size("dp")
    return lax.ppermute(block, "dp", [(i, i ^ 1) for i in range(count)])


def split_body(count, q_lead, skip, p_ref, x_ref, *refs):
    outs, held = refs[:count], refs[count]
    n_lead = p_ref.shape[1]
    q = held.shape[1] - q_lead
    for g in range(count):
        n = max(0, min(q_lead, n_lead - g * q_lead))
        if n < q_lead:
            held[g] = jnp.zeros(held.shape[1:], BF16)
        if n:
            held[g, :n, :] = p_ref[0, g * q_lead : g * q_lead + n, :]
        held[g, q_lead:, :] = x_ref[0, skip + g * q : skip + (g + 1) * q, :]
    me = lax.axis_index("dp") // PAIR
    for k in range(count):
        outs[k][...] = held[partner(me, k, count)]


def spread_body(count, tp, *refs):
    n = block_count(tp)
    blocks, outs, held = refs[:n], refs[n : n + count], refs[-1]
    q = outs[0].shape[1]
    gather_blocks(tp, blocks, held)
    me = lax.axis_index("dp") // PAIR
    for k in range(count):
        p = partner(me, k, count)
        for g in range(count):

            @pl.when(p == g)
            def _(k=k, g=g):
                outs[k][...] = held[:, g * q : (g + 1) * q, :]


def gather_blocks(tp, blocks, held, at=0):
    rows = blocks[0].shape[0]
    me = lax.axis_index("tensor")
    for j in range(tp):
        for i in range(tp):
            source = blocks[holds(tp, i, j)]

            @pl.when(me == i)
            def _(j=j, source=source):
                held[j, at : at + rows, :] = source[...]


def find(slot, values, place, count):
    found = jnp.int32(0)
    for e in range(count):
        found = jnp.where(slot[e] == place, e if values is None else values[e], found)
    return found


def choose_body(count, examples, q_lead, slot, task_of, *refs):
    own, sib, outs = refs[:count], refs[count : 2 * count], refs[2 * count : 3 * count]
    held = refs[3 * count]
    index = lax.axis_index("dp")
    me, core = index // PAIR, lax.rem(index, PAIR)
    for k in range(count):
        held[k] = own[k][...]
        held[count + k] = sib[k][...]

    def where_is(e):
        return step_of(e // PAIR, me, count) + jnp.where(lax.rem(e, PAIR) == core, 0, count)

    for k in range(count):
        place = partner(me, k, count) * PAIR + core
        at = where_is(find(slot, None, place, examples))
        if q_lead:
            outs[k][q_lead:] = held[at, q_lead:]
            outs[k][:q_lead] = held[where_is(find(slot, task_of, place, examples)), :q_lead]
        else:
            outs[k][...] = held[at]


def place_rows(pieces, slot, task_of, q_lead):
    count = len(pieces)
    shape = pieces[0].shape
    got = to_groups(pieces)
    sib = [to_sibling(b) for b in got]
    chosen = call(
        functools.partial(choose_body, count, slot.shape[0], q_lead),
        [(shape, BF16)] * count,
        [SM, SM] + [VM] * (2 * count),
        [slot, task_of, *got, *sib],
        [pltpu.VMEM((2 * count,) + shape, BF16)],
    )
    return to_groups(chosen)


def join_body(count, cuts, *refs):
    ins, outs, held = refs[:count], refs[count : count + len(cuts)], refs[-1]
    me = lax.axis_index("dp") // PAIR
    for k in range(count):
        held[came_from(me, k, count)] = ins[k][...]
    for out, (low, high, rows) in zip(outs, cuts):
        q = high - low
        for g in range(count):
            n = max(0, min(q, rows - g * q))
            if n and len(ins[0].shape) == 3:
                out[:, g * q : g * q + n, :] = held[g, :, low : low + n, :]
            elif n and len(out.shape) == 3:
                out[0, g * q : g * q + n, :] = held[g, low : low + n, :].astype(out.dtype)
            elif n:
                out[g * q : g * q + n, :] = held[g, low : low + n, :].astype(out.dtype)


def join_rows(pieces, cuts, dtype=BF16, lead=()):
    count = len(pieces)
    shape = pieces[0].shape
    return call(
        functools.partial(join_body, count, cuts),
        [(lead + (rows, shape[-1]), dtype) for _, _, rows in cuts],
        [VM] * count,
        pieces,
        [pltpu.VMEM((count,) + shape, BF16)],
    )


def holds(tp, i, j):
    if tp != 4:
        return i - j if i >= j else tp - 1 + j - i
    return i ^ j if i ^ j < 3 else 3 + int(i in (0, tp - 1))


def block_count(tp):
    return 5 if tp == 4 else 2 * tp - 1


def chain_gather(block, axis):
    tp = lax.axis_size(axis)

    def move(value, pairs):
        return lax.ppermute(value, axis, pairs)

    if tp == 4:
        far = move(block, [(i, i ^ 2) for i in range(4)])
        pair = move(block, [(i, i ^ 1) for i in range(4)])
        mid = move(block, [(1, 2), (2, 1)])
        passed = move(far, [(1, 0), (2, 3)])
        return [block, pair, far, mid, passed]
    from_left, from_right = [block], [block]
    for hop in range(1, tp):
        right = [(i, i + 1) for i in range(hop - 1, tp - 1)]
        left = [(i, i - 1) for i in range(1, tp - hop + 1)]
        from_left.append(move(from_left[-1], right))
        from_right.append(move(from_right[-1], left))
    return [block, *from_left[1:], *from_right[1:]]


def spin(x, cosine, sine):
    return x * cosine + pltpu.roll(x, HD // 2, 1) * sine


def nt(a, b):
    return lax.dot_general(a, b, (((1,), (1,)), ((), ())), preferred_element_type=F32)


def tn(a, b):
    return lax.dot_general(a, b, (((0,), (0,)), ((), ())), preferred_element_type=F32)


def chunk_body(cfg, *refs):
    refs = list(refs)

    def take(n):
        out = refs[:n]
        del refs[:n]
        return out

    tp, first, last = cfg["tp"], cfg["first"], cfg["last"]
    rows, lead, lead_pad = cfg["rows"], cfg["lead"], cfg["lead_pad"]
    prompt_len, keys_pad, start = cfg["prompt_len"], cfg["keys_pad"], cfg["start"]
    width, heads, prior = cfg["width"], cfg["heads"], cfg["prior"]
    depth, cols = tp * width, heads * HD
    slot, lengths, gain = take(3)
    weights = take(3)
    cosine, sine, cot = take(3)
    segments = [take(block_count(tp) if chained else 1) for chained, _ in cfg["segments"]]
    before = [take(2) for _ in prior]
    if not first:
        gk_in, gv_in = take(2)
    if last:
        inv_lead, flat_lead, dot_lead = take(3)
    (out,) = take(1)
    if last:
        turned, pull_out = take(2)
    else:
        k_out, v_out, gk_out, gv_out = take(4)
        if first:
            x_out, inv_out, flat_out, dot_out, turned = take(5)
    x_buf, n_buf, acc, k_all, v_all = take(5)
    if last:
        gk_out, gv_out = take(2)

    def weight(m, j):
        return weights[m][pl.ds(pl.multiple_of(j * width, width), width), :]

    at = 0
    for blocks, (chained, n) in zip(segments, cfg["segments"]):
        if chained:
            gather_blocks(tp, blocks, x_buf, at)
        else:
            x_buf[:, at : at + n, :] = blocks[0][...]
        at += n
    square = jnp.zeros((rows, 1), F32)
    for j in range(tp):
        wide = x_buf[j].astype(F32)
        square = square + jnp.sum(wide * wide, axis=1, keepdims=True)
    inv_rms = lax.rsqrt(square / depth + 1e-05)
    for j in range(tp):
        n_buf[j] = (x_buf[j].astype(F32) * inv_rms * gain[j]).astype(BF16)
    if first:
        x_out[...] = x_buf[:, :lead, :]
        inv_out[...] = jnp.broadcast_to(inv_rms[:lead], (lead, HD))
    acc[...] = jnp.zeros_like(acc)

    def project(j, _):
        for m in range(3):
            acc[m] += jnp.dot(n_buf[j], weight(m, j), preferred_element_type=F32)
        return 0

    lax.fori_loop(0, tp, project, 0)
    length = find(slot, lengths, lax.axis_index("dp"), cfg["examples"])
    limit = lead + length
    at = 0
    for (k_ref, v_ref), n in zip(before, prior):
        k_all[at : at + n, :] = k_ref[...]
        v_all[at : at + n, :] = v_ref[...]
        at += n
    if keys_pad > at + rows:
        k_all[at + rows :, :] = jnp.zeros((keys_pad - at - rows, cols), BF16)
        v_all[at + rows :, :] = jnp.zeros((keys_pad - at - rows, cols), BF16)
    cos, sin = cosine[start : start + rows, :], sine[start : start + rows, :]
    scale = 1.0 / math.sqrt(HD)
    r = lax.broadcasted_iota(jnp.int32, (rows, keys_pad), 0) + start
    c = lax.broadcasted_iota(jnp.int32, (rows, keys_pad), 1)
    allowed = (c <= r) & ((c < prompt_len) | (c >= lead)) & (c < limit)
    live = lax.broadcasted_iota(jnp.int32, (rows, HD), 0) + start < limit
    dot = jnp.zeros((rows, 1), F32)
    for h in range(heads):
        s = slice(h * HD, (h + 1) * HD)
        q = spin(acc[0, :, s], cos, sin).astype(BF16)
        k_all[at : at + rows, s] = spin(acc[1, :, s], cos, sin).astype(BF16)
        v_all[at : at + rows, s] = acc[2, :, s].astype(BF16)
        k, v = k_all[:, s], v_all[:, s]
        scores = jnp.where(allowed, nt(q, k) * scale, -1e30)
        peak = jnp.max(scores, axis=1, keepdims=True)
        w = jnp.exp(scores - peak)
        prob = w * (1.0 / jnp.sum(w, axis=1, keepdims=True))
        low = prob.astype(BF16)
        mixed = jnp.dot(low, v, preferred_element_type=F32)
        out[:, s] = jnp.where(live, mixed, 0.0).astype(BF16)
        up = jnp.where(live, cot[:, s].astype(F32), 0.0).astype(BF16)
        grad_prob = nt(up, v)
        delta = jnp.sum(prob * grad_prob, axis=1, keepdims=True)
        score = (prob * (grad_prob - delta)).astype(BF16)
        gk = tn(score[:, :lead_pad], q)
        gv = tn(low[:, :lead_pad], up)
        if first:
            gk_out[:, s] = gk
            gv_out[:, s] = gv
            gq = jnp.dot(score, k, preferred_element_type=F32) * scale
            gq = spin(gq, cos, -sin).astype(BF16).astype(F32)
            dot = dot + jnp.sum(gq * acc[0, :, s], axis=1, keepdims=True)
            gq = jnp.concatenate([gq, jnp.zeros((lead_pad - lead, HD), F32)], axis=0)
            turned[s, :] = gq.T.astype(BF16)
        else:
            gk_out[:, s] = gk_in[:, s] + gk
            gv_out[:, s] = gv_in[:, s] + gv
    if first:
        flat_out[...] = acc[1:]
        dot_out[...] = jnp.broadcast_to(dot, (rows, HD))
    if not last:
        k_out[...] = k_all[at : at + rows, :]
        v_out[...] = v_all[at : at + rows, :]
        return
    cos, sin = cosine[:lead_pad, :], sine[:lead_pad, :]
    dot = dot_lead[:, :1]
    for h in range(heads):
        s = slice(h * HD, (h + 1) * HD)
        gk = spin(gk_out[:, s] * scale, cos, -sin).astype(BF16).astype(F32)
        gv = gv_out[:, s].astype(BF16).astype(F32)
        dot = dot + jnp.sum(gk[:lead] * flat_lead[0, :, s], axis=1, keepdims=True)
        dot = dot + jnp.sum(gv[:lead] * flat_lead[1, :, s], axis=1, keepdims=True)
        turned[0, s, :] = gk.T.astype(BF16)
        turned[1, s, :] = gv.T.astype(BF16)
    inv = inv_lead[:, :1]
    pull_out[...] = jnp.broadcast_to(inv * inv * (dot / depth), (lead, HD))


def back_body(tp, k, gain, wq, wk, wv, x_lead, inv_lead, pull, turned_q, turned, out):
    lead, width = out.shape
    to = partner(lax.axis_index("tensor"), k, tp)
    at = pl.ds(pl.multiple_of(to * width, width), width)
    gn = jnp.dot(wq[at, :], turned_q[...], preferred_element_type=F32)
    gn = gn + jnp.dot(wk[at, :], turned[0], preferred_element_type=F32)
    gn = gn + jnp.dot(wv[at, :], turned[1], preferred_element_type=F32)
    gn = gn.T[:lead] * gain[to]
    out[...] = (inv_lead[:, :1] * gn - x_lead[to].astype(F32) * pull[:, :1]).astype(BF16)


def sum_body(count, n, *refs):
    ins, outs, whole, held = refs[:n], refs[n : n + count], refs[n + count], refs[n + count + 1]
    rows, q = ins[0].shape[0], outs[0].shape[0]
    total = ins[0][...].astype(F32)
    for i in range(1, n):
        total = total + ins[i][...].astype(F32)
    whole[...] = total.astype(BF16)
    for g in range(count):
        m = max(0, min(q, rows - g * q))
        if m < q:
            held[g] = jnp.zeros(held.shape[1:], BF16)
        if m:
            held[g, :m, :] = whole[g * q : g * q + m, :]
    me = lax.axis_index("dp") // PAIR
    for k in range(count):
        outs[k][...] = held[partner(me, k, count)]


def collect_body(count, examples, slot, task_of, *refs):
    ins, mine, other = refs[:count], refs[count], refs[count + 1]
    index = lax.axis_index("dp")
    me, core = index // PAIR, lax.rem(index, PAIR)
    tasks = []
    for k in range(count):
        place = came_from(me, k, count) * PAIR + core
        tasks.append(find(slot, task_of, place, examples))
    for g in range(count):
        for target, side in ((mine, core), (other, 1 - core)):
            total = jnp.zeros(ins[0].shape, F32)
            for k in range(count):
                share = jnp.where(tasks[k] == g * PAIR + side, 1.0, 0.0)
                total = total + share * ins[k][...].astype(F32)
            target[g] = total.astype(target.dtype)


def finish_body(count, mine, other, *outs):
    me = lax.axis_index("dp") // PAIR
    for k in range(count):
        p = partner(me, k, count)
        outs[k][...] = (mine[p] + other[p].astype(F32)).astype(BF16)


def on_device(text, prompts, gain, w_query, w_key, w_value, cotangent, task_of, lengths, slot):
    count = lax.axis_size("dp") // PAIR
    tp = lax.axis_size("tensor")
    prompt_len, text_len, width = prompts.shape[1], text.shape[1], text.shape[2]
    examples = slot.shape[0]
    cols = w_query.shape[1]
    heads = cols // HD
    lead = up_to(prompt_len, 8)
    lead_pad = up_to(lead, 128)
    early = text_len // 2
    late = text_len - early
    prompt_q = up_to(-(-prompt_len // count), 16)
    late_q, early_q = late // count, early // count
    wide = chain_gather(text[0, :early], "tensor")
    piece = (prompt_q + late_q, width)
    pieces = call(
        functools.partial(split_body, count, prompt_q, early),
        [(piece, BF16)] * count,
        [VM, VM],
        [prompts, text],
        [pltpu.VMEM((count,) + piece, BF16)],
    )
    placed = place_rows(pieces, slot, task_of, prompt_q)
    cuts = [(0, prompt_q, lead), (prompt_q, prompt_q + late_q, late)]
    rows_a, rows_c = join_rows(placed, cuts)
    chain_a = chain_gather(rows_a, "tensor")
    chain_c = chain_gather(rows_c, "tensor")
    wide_pieces = call(
        functools.partial(spread_body, count, tp),
        [((tp, early_q, width), BF16)] * count,
        [VM] * len(wide),
        wide,
        [pltpu.VMEM((tp, early, width), BF16)],
    )
    wide_placed = place_rows(wide_pieces, slot, task_of, 0)
    (rows_b,) = join_rows(wide_placed, [(0, early_q, early)], BF16, (tp,))

    at = jnp.arange(lead + text_len, dtype=jnp.int32)
    at = jnp.where(at < lead, at, at - (lead - prompt_len)).astype(F32)
    frequency = 10000.0 ** (-jnp.arange(HD // 2, dtype=F32) / (HD // 2))
    angle = at[:, None] * frequency[None, :]
    cosine, sine = jnp.cos(angle), jnp.sin(angle)
    cosine = jnp.concatenate([cosine, cosine], axis=1)
    sine = jnp.concatenate([-sine, sine], axis=1)
    gain_rows = gain.reshape(tp, 1, width)
    split_at = prompt_len + early
    cots = [
        jnp.pad(cotangent[0, :prompt_len], ((0, lead - prompt_len), (0, 0))),
        cotangent[0, prompt_len:split_at],
        cotangent[0, split_at:],
    ]
    chunks = [
        ([(True, lead)], chain_a),
        ([(False, early)], [rows_b]),
        ([(True, late)], chain_c),
    ]
    outputs, before, grads, saved, start = [], [], [], [], 0
    for i, (segments, blocks) in enumerate(chunks):
        first, last = i == 0, i == len(chunks) - 1
        rows = cots[i].shape[0]
        keys_pad = up_to(start + rows, 128)
        cfg = dict(
            tp=tp, first=first, last=last, rows=rows, lead=lead, lead_pad=lead_pad,
            prompt_len=prompt_len, keys_pad=keys_pad, start=start, width=width, heads=heads,
            prior=[k.shape[0] for k, _ in before], examples=examples, segments=segments,
        )
        args = [slot, lengths, gain_rows, w_query, w_key, w_value, cosine, sine, cots[i]]
        specs = [SM, SM] + [VM] * 7
        extra = list(blocks)
        for pair in before:
            extra += pair
        extra += grads + (saved[1:4] if last else [])
        outs = [((rows, cols), BF16)]
        scratch = [
            pltpu.VMEM((tp, rows, width), BF16),
            pltpu.VMEM((tp, rows, width), BF16),
            pltpu.VMEM((3, rows, cols), F32),
            pltpu.VMEM((keys_pad, cols), BF16),
            pltpu.VMEM((keys_pad, cols), BF16),
        ]
        if last:
            outs += [((2, cols, lead_pad), BF16), ((lead, HD), F32)]
            scratch += [pltpu.VMEM((lead_pad, cols), F32)] * 2
        else:
            outs += [((rows, cols), BF16)] * 2 + [((lead_pad, cols), F32)] * 2
            if first:
                outs += [((tp, lead, width), BF16), ((lead, HD), F32), ((2, lead, cols), F32)]
                outs += [((lead, HD), F32), ((cols, lead_pad), BF16)]
        got = call(
            functools.partial(chunk_body, cfg),
            outs,
            specs + [VM] * len(extra),
            args + extra,
            scratch,
            flops=2 * rows * tp * width * 3 * cols,
        )
        outputs.append(got[0])
        if last:
            turned, pull = got[1:]
        else:
            before.append((got[1], got[2]))
            grads = [got[3], got[4]]
            if first:
                saved = list(got[5:])
        start += rows
    output = jnp.concatenate([outputs[0][:prompt_len], *outputs[1:]], axis=0)[None]

    x_lead, inv_lead, _, _, turned_q = saved
    got = []
    for k in reversed(range(tp)):
        (block,) = call(
            functools.partial(back_body, tp, k),
            [((lead, width), BF16)],
            [VM] * 9,
            [gain_rows, w_query, w_key, w_value, x_lead, inv_lead, pull, turned_q, turned],
        )
        if k:
            pairs = [(i, i ^ k if tp & (tp - 1) == 0 else (i + k) % tp) for i in range(tp)]
            block = lax.ppermute(block, "tensor", pairs)
        got.append(block)
    pieces = call(
        functools.partial(sum_body, count, tp),
        [((prompt_q, width), BF16)] * count,
        [VM] * tp,
        got,
        [pltpu.VMEM((lead, width), BF16), pltpu.VMEM((count, prompt_q, width), BF16)],
    )
    mine, other = call(
        functools.partial(collect_body, count, examples),
        [((count, prompt_q, width), F32), ((count, prompt_q, width), BF16)],
        [SM, SM] + [VM] * count,
        [slot, task_of, *to_groups(pieces)],
    )
    done = call(
        functools.partial(finish_body, count),
        [((prompt_q, width), BF16)] * count,
        [VM, VM],
        [mine, to_sibling(other)],
    )
    (prompt_grad,) = join_rows(to_groups(done), [(0, prompt_q, prompt_len)], F32, (1,))
    return (output, prompt_grad)


def solution(mesh):
    in_specs = (
        P("dp", None, "tensor"),
        P("dp", None, "tensor"),
        P(),
        P(None, "tensor"),
        P(None, "tensor"),
        P(None, "tensor"),
        P("dp", None, "tensor"),
        P(),
        P(),
        P(),
    )
    out_specs = (P("dp", None, "tensor"), P("dp", None, "tensor"))
    return jax.shard_map(
        on_device, mesh=mesh, in_specs=in_specs, out_specs=out_specs, check_vma=False
    )
```

profile of v0, /device:TPU:0, one launch (start us, length us, event | category | flops | bytes accessed | tf_op | source)
XLA Modules:
  0.0 156.7 jit_solution(1600448179765794586)
XLA Ops:
  0.6 1.1 slice_bitcast_fusion.refs_0_
  1.8 4.1 %collective-permute-start.15 = (bf16[128,1280]{1,0:T(8,128)(2,1)S(1)}, bf16[128,1280]{1,0:T(8,128)(2,1)S(1)}, u32[]{:S(2)}, u32[]{:S(2)}) collective-permute-start(bf16[128,1280]{1,0:T(8,128)(2,1)S(1)} %slice_bitcast_fusion.refs_0_), channel_id=1, source_target_pairs={{0,2},{1,3},{2,0},{3,1},{4,6},{5,7},{6,4},{7,5},{8,10},{9,11},{10,... | collective-permute-start | bytes 983048 | tf_op jit(solution)/shard_map/ppermute | solution.py:205
  5.9 1.1 copy-done.3
  8.1 1.6 collective-permute-start
  9.6 1.5 collective-permute-start.1
  11.6 3.3 %collective-permute-done.refs_1_ = bf16[64,1280]{1,0:T(8,128)(2,1)S(1)} collective-permute-done((bf16[64,1280]{1,0:T(8,128)(2,1)S(1)}, bf16[64,1280]{1,0:T(8,128)(2,1)S(1)}, u32[]{:S(2)}, u32[]{:S(2)}) %collective-permute-start) | collective-permute-done | bytes 163872 | tf_op jit(solution)/shard_map/ppermute | solution.py:66
  14.9 3.6 %collective-permute-done.1.refs_2_ = bf16[64,1280]{1,0:T(8,128)(2,1)S(1)} collective-permute-done((bf16[64,1280]{1,0:T(8,128)(2,1)S(1)}, bf16[64,1280]{1,0:T(8,128)(2,1)S(1)}, u32[]{:S(2)}, u32[]{:S(2)}) %collective-permute-start.1) | collective-permute-done | bytes 163872 | tf_op jit(solution)/shard_map/ppermute | solution.py:66
  18.5 1.6 %collective-permute-start.14 = (bf16[128,1280]{1,0:T(8,128)(2,1)S(1)}, bf16[128,1280]{1,0:T(8,128)(2,1)S(1)}, u32[]{:S(2)}, u32[]{:S(2)}) collective-permute-start(bf16[128,1280]{1,0:T(8,128)(2,1)S(1)} %slice_bitcast_fusion.refs_0_), channel_id=1, source_target_pairs={{0,1},{1,0},{2,3},{3,2},{4,5},{5,4},{6,7},{7,6},{8,9},{9,8},{10,11... | collective-permute-start | bytes 983048 | tf_op jit(solution)/shard_map/ppermute | solution.py:205
  20.9 1.3 collective-permute-start.17
  24.4 1.4 collective-permute-start.7
  25.8 1.5 collective-permute-start.8
  27.3 1.7 %collective-permute-done.14.refs_1_ = bf16[128,1280]{1,0:T(8,128)(2,1)S(1)} collective-permute-done((bf16[128,1280]{1,0:T(8,128)(2,1)S(1)}, bf16[128,1280]{1,0:T(8,128)(2,1)S(1)}, u32[]{:S(2)}, u32[]{:S(2)}) %collective-permute-start.14) | collective-permute-done | bytes 327712 | tf_op jit(solution)/shard_map/ppermute | solution.py:205
  29.1 1.5 collective-permute-start.9
  30.6 4.1 %collective-permute-done.17.refs_4_ = bf16[128,1280]{1,0:T(8,128)(2,1)S(1)} collective-permute-done((bf16[128,1280]{1,0:T(8,128)(2,1)S(1)}, bf16[128,1280]{1,0:T(8,128)(2,1)S(1)}, u32[]{:S(2)}, u32[]{:S(2)}) %collective-permute-start.17) | collective-permute-done | bytes 327712 | tf_op jit(solution)/shard_map/ppermute | solution.py:205
  35.0 1.6 %collective-permute-start.18 = (bf16[4,32,1280]{2,1,0:T(8,128)(2,1)S(1)}, bf16[4,32,1280]{2,1,0:T(8,128)(2,1)S(1)}, u32[]{:S(2)}, u32[]{:S(2)}) collective-permute-start(bf16[4,32,1280]{2,1,0:T(8,128)(2,1)S(1)} %get-tuple-element.59), channel_id=1, source_target_pairs={{0,8},{4,12},{8,0},{12,4},{16,24},{20,28},{24,16},{28,20},{1,9},{5... | collective-permute-start | bytes 983048 | tf_op jit(solution)/shard_map/ppermute | solution.py:66
  36.6 1.5 collective-permute-start.19
  38.8 1.7 %collective-permute-start.11 = (bf16[104,1280]{1,0:T(8,128)(2,1)S(1)}, bf16[104,1280]{1,0:T(8,128)(2,1)S(1)}, u32[]{:S(2)}, u32[]{:S(2)}) collective-permute-start(bf16[104,1280]{1,0:T(8,128)(2,1)S(1)} %get-tuple-element.56.refs_9_), channel_id=1, source_target_pairs={{0,2},{1,3},{2,0},{3,1},{4,6},{5,7},{6,4},{7,5},{8,10},{9,11},{10,... | collective-permute-start | bytes 798728 | tf_op jit(solution)/shard_map/ppermute | solution.py:205
  40.5 5.2 %collective-permute-done.18.refs_1_ = bf16[4,32,1280]{2,1,0:T(8,128)(2,1)S(1)} collective-permute-done((bf16[4,32,1280]{2,1,0:T(8,128)(2,1)S(1)}, bf16[4,32,1280]{2,1,0:T(8,128)(2,1)S(1)}, u32[]{:S(2)}, u32[]{:S(2)}) %collective-permute-start.18) | collective-permute-done | bytes 327712 | tf_op jit(solution)/shard_map/ppermute | solution.py:66
  45.7 7.3 %collective-permute-done.19.refs_2_ = bf16[4,32,1280]{2,1,0:T(8,128)(2,1)S(1)} collective-permute-done((bf16[4,32,1280]{2,1,0:T(8,128)(2,1)S(1)}, bf16[4,32,1280]{2,1,0:T(8,128)(2,1)S(1)}, u32[]{:S(2)}, u32[]{:S(2)}) %collective-permute-start.19) | collective-permute-done | bytes 327712 | tf_op jit(solution)/shard_map/ppermute | solution.py:66
  55.0 1.3 collective-permute-start.13
  56.4 5.3 %collective-permute-start.29 = (bf16[128,1280]{1,0:T(8,128)(2,1)S(1)}, bf16[128,1280]{1,0:T(8,128)(2,1)S(1)}, u32[]{:S(2)}, u32[]{:S(2)}) collective-permute-start(bf16[128,1280]{1,0:T(8,128)(2,1)S(1)} %get-tuple-element.71.refs_9_), channel_id=1, source_target_pairs={{0,2},{1,3},{2,0},{3,1},{4,6},{5,7},{6,4},{7,5},{8,10},{9,11},{10,... | collective-permute-start | bytes 983048 | tf_op jit(solution)/shard_map/ppermute | solution.py:205
  63.3 1.3 collective-permute-start.26
  64.7 1.4 collective-permute-start.27
  66.3 2.0 %collective-permute-done.13.refs_13_ = bf16[104,1280]{1,0:T(8,128)(2,1)S(1)} collective-permute-done((bf16[104,1280]{1,0:T(8,128)(2,1)S(1)}, bf16[104,1280]{1,0:T(8,128)(2,1)S(1)}, u32[]{:S(2)}, u32[]{:S(2)}) %collective-permute-start.13) | collective-permute-done | bytes 266272 | tf_op jit(solution)/shard_map/ppermute | solution.py:205
  68.3 8.5 %collective-permute-start.28 = (bf16[128,1280]{1,0:T(8,128)(2,1)S(1)}, bf16[128,1280]{1,0:T(8,128)(2,1)S(1)}, u32[]{:S(2)}, u32[]{:S(2)}) collective-permute-start(bf16[128,1280]{1,0:T(8,128)(2,1)S(1)} %get-tuple-element.71.refs_9_), channel_id=1, source_target_pairs={{0,1},{1,0},{2,3},{3,2},{4,5},{5,4},{6,7},{7,6},{8,9},{9,8},{10,11... | collective-permute-start | bytes 983048 | tf_op jit(solution)/shard_map/ppermute | solution.py:205
  76.8 3.2 %copy-done = bf16[5120,768]{1,0:T(8,128)(2,1)S(1)} copy-done((bf16[5120,768]{1,0:T(8,128)(2,1)S(1)}, bf16[5120,768]{1,0:T(8,128)(2,1)}, u32[]{:S(2)}) %copy-start) | copy-done | bytes 7864344
  80.1 9.3 %shard_map.116 = (bf16[104,768]{1,0:T(8,128)(2,1)S(1)}, bf16[104,768]{1,0:T(8,128)(2,1)S(1)}, bf16[104,768]{1,0:T(8,128)(2,1)S(1)}, f32[128,768]{1,0:T(8,128)S(1...) custom-call(s32[8]{0:T(128)S(1)} %copy-done.5, ...), custom_call_target="tpu_custom_call" | custom-call | flops 2453667840 | bytes 1048576 | tf_op jit(solution)/shard_map/pallas_call | solution.py:27
  90.0 1.5 collective-permute-start.31
  91.8 6.7 %shard_map.120 = (bf16[128,768]{1,0:T(8,128)(2,1)S(1)}, bf16[128,768]{1,0:T(8,128)(2,1)S(1)}, bf16[128,768]{1,0:T(8,128)(2,1)S(1)}, f32[128,768]{1,0:T(8,128)S(1)}, f32[128,768]{1,0:T(8,128)S(1)}) custom-call(s32[8]{0:T(128)S(1)} %copy-done.5, s32[8]{0:T(128)S(1)} %copy-done.4, f32[4,1,1280]{2,1,0:T(1,128)S(1)} %bitcast.17, bf16[5120,768]{1,0:T(8,128)(2,1)S(1)} %bitcast.13, ...), custom_call_target="tpu_custom_call" | custom-call | flops 3019898880 | bytes 1048576 | tf_op jit(solution)/shard_map/pallas_call | solution.py:27
  98.5 1.1 collective-permute-done.31.refs_13_
  99.7 9.7 %shard_map.121 = (bf16[128,768]{1,0:T(8,128)(2,1)S(1)}, bf16[2,768,128]{2,1,0:T(8,128)(2,1)S(1)}, f32[104,128]{1,0:T(8,128)S(1)}) custom-call(s32[8]{0:T(128)S(1)} %copy-done.5, s32[8]{0:T(128)S(1)} %copy-done.4, f32[4,1,1280]{2,1,0:T(1,128)S(1)} %bitcast.18, bf16[5120,768]{1,0:T(8,128)(2,1)S(1)} %bitcast.13, bf16[5120,768]{1,0:T(8,128)(2,1)S(1)} %bitcast.15, ...), custom_call_target="tpu_custom_call" | custom-call | flops 3019898880 | bytes 1048576 | tf_op jit(solution)/shard_map/pallas_call | solution.py:27
  109.4 1.8 %shard_map.124 = bf16[104,1280]{1,0:T(8,128)(2,1)S(1)} custom-call(f32[4,1,1280]{2,1,0:T(1,128)S(1)} %bitcast.19, bf16[5120,768]{1,0:T(8,128)(2,1)S(1)} %bitcast.13, bf16[5120,768]{1,0:T(8,128)(2,1)S(1)} %bitcast.15, bf16[5120,768]{1,0:T(8,128)(2,1)S(1)} %copy-done.1, bf16[4,104,1280]{2,1,0:T(8,128)(2,1)S(1)} %get-tuple-element.80.x_lead, ...), custom_call_target="tpu_custom_call" | custom-call | flops 1000000000 | bytes 1048576 | tf_op jit(solution)/shard_map/pallas_call | solution.py:27
  111.2 1.8 %shard_map.123 = bf16[104,1280]{1,0:T(8,128)(2,1)S(1)} custom-call(f32[4,1,1280]{2,1,0:T(1,128)S(1)} %bitcast.20, bf16[5120,768]{1,0:T(8,128)(2,1)S(1)} %bitcast.13, bf16[5120,768]{1,0:T(8,128)(2,1)S(1)} %bitcast.15, bf16[5120,768]{1,0:T(8,128)(2,1)S(1)} %copy-done.1, bf16[4,104,1280]{2,1,0:T(8,128)(2,1)S(1)} %get-tuple-element.80.x_lead, ...), custom_call_target="tpu_custom_call" | custom-call | flops 1000000000 | bytes 1048576 | tf_op jit(solution)/shard_map/pallas_call | solution.py:27
  113.0 1.8 %shard_map.122 = bf16[104,1280]{1,0:T(8,128)(2,1)S(1)} custom-call(f32[4,1,1280]{2,1,0:T(1,128)S(1)} %bitcast.21, bf16[5120,768]{1,0:T(8,128)(2,1)S(1)} %bitcast.13, bf16[5120,768]{1,0:T(8,128)(2,1)S(1)} %bitcast.15, bf16[5120,768]{1,0:T(8,128)(2,1)S(1)} %copy-done.1, bf16[4,104,1280]{2,1,0:T(8,128)(2,1)S(1)} %get-tuple-element.80.x_lead, ...), custom_call_target="tpu_custom_call" | custom-call | flops 1000000000 | bytes 1048576 | tf_op jit(solution)/shard_map/pallas_call | solution.py:27
  114.8 2.2 %collective-permute-start.34 = (bf16[104,1280]{1,0:T(8,128)(2,1)S(1)}, bf16[104,1280]{1,0:T(8,128)(2,1)S(1)}, u32[]{:S(2)}, u32[]{:S(2)}) collective-permute-start(bf16[104,1280]{1,0:T(8,128)(2,1)S(1)} %shard_map.124), channel_id=1, source_target_pairs={{0,1},{1,0},{2,3},{3,2},{4,5},{5,4},{6,7},{7,6},{8,9},{9,8},{10,11... | collective-permute-start | bytes 798728 | tf_op jit(solution)/shard_map/ppermute | solution.py:534
  117.8 1.6 %collective-permute-start.32 = (bf16[104,1280]{1,0:T(8,128)(2,1)S(1)}, bf16[104,1280]{1,0:T(8,128)(2,1)S(1)}, u32[]{:S(2)}, u32[]{:S(2)}) collective-permute-start(bf16[104,1280]{1,0:T(8,128)(2,1)S(1)} %shard_map.122), channel_id=1, source_target_pairs={{0,3},{1,2},{2,1},{3,0},{4,7},{5,6},{6,5},{7,4},{8,11},{9,10},{10,... | collective-permute-start | bytes 798728 | tf_op jit(solution)/shard_map/ppermute | solution.py:534
  119.4 1.8 %shard_map.125.refs_3_ = bf16[104,1280]{1,0:T(8,128)(2,1)S(1)} custom-call(f32[4,1,1280]{2,1,0:T(1,128)S(1)} %bitcast.22, bf16[5120,768]{1,0:T(8,128)(2,1)S(1)} %bitcast.13, bf16[5120,768]{1,0:T(8,128)(2,1)S(1)} %bitcast.15, bf16[5120,768]{1,0:T(8,128)(2,1)S(1)} %copy-done.1, bf16[4,104,1280]{2,1,0:T(8,128)(2,1)S(1)} %get-tuple-element.80.x_lead, ...), custom_call_target="tpu_custom_call" | custom-call | flops 1000000000 | bytes 1048576 | tf_op jit(solution)/shard_map/pallas_call | solution.py:27
  121.2 2.9 %collective-permute-done.34.refs_2_ = bf16[104,1280]{1,0:T(8,128)(2,1)S(1)} collective-permute-done((bf16[104,1280]{1,0:T(8,128)(2,1)S(1)}, bf16[104,1280]{1,0:T(8,128)(2,1)S(1)}, u32[]{:S(2)}, u32[]{:S(2)}) %collective-permute-start.34) | collective-permute-done | bytes 266272 | tf_op jit(solution)/shard_map/ppermute | solution.py:534
  124.1 12.9 %collective-permute-done.33.refs_1_ = bf16[104,1280]{1,0:T(8,128)(2,1)S(1)} collective-permute-done((bf16[104,1280]{1,0:T(8,128)(2,1)S(1)}, bf16[104,1280]{1,0:T(8,128)(2,1)S(1)}, u32[]{:S(2)}, u32[]{:S(2)}) %collective-permute-start.33) | collective-permute-done | bytes 266272 | tf_op jit(solution)/shard_map/ppermute | solution.py:534
  137.2 1.5 collective-permute-start.35
  139.2 1.6 collective-permute-start.37
  141.8 1.4 collective-permute-done.36.refs_2_
  143.2 1.4 collective-permute-done.37.refs_3_
  145.7 1.6 %collective-permute-done.38.other = bf16[4,32,1280]{2,1,0:T(8,128)(2,1)S(1)} collective-permute-done((bf16[4,32,1280]{2,1,0:T(8,128)(2,1)S(1)}, bf16[4,32,1280]{2,1,0:T(8,128)(2,1)S(1)}, u32[]{:S(2)}, u32[]{:S(2)}) %collective-permute-start.38) | collective-permute-done | bytes 327712 | tf_op jit(solution)/shard_map/ppermute | solution.py:72
  147.4 1.8 %collective-permute-start.39 = (bf16[32,1280]{1,0:T(8,128)(2,1)S(1)}, bf16[32,1280]{1,0:T(8,128)(2,1)S(1)}, u32[]{:S(2)}, u32[]{:S(2)}) collective-permute-start(bf16[32,1280]{1,0:T(8,128)(2,1)S(1)} %get-tuple-element.91), channel_id=1, source_target_pairs={{0,8},{4,12},{8,0},{12,4},{16,24},{20,28},{24,16},{28,20},{1,9},{5... | collective-permute-start | bytes 245768 | tf_op jit(solution)/shard_map/ppermute | solution.py:66
  149.6 1.4 collective-permute-start.41
  152.0 3.4 %collective-permute-done.40.refs_2_ = bf16[32,1280]{1,0:T(8,128)(2,1)S(1)} collective-permute-done((bf16[32,1280]{1,0:T(8,128)(2,1)S(1)}, bf16[32,1280]{1,0:T(8,128)(2,1)S(1)}, u32[]{:S(2)}, u32[]{:S(2)}) %collective-permute-start.40) | collective-permute-done | bytes 81952 | tf_op jit(solution)/shard_map/ppermute | solution.py:66
  155.4 1.3 copy.12
  (91 shorter events, 15.5 us)
Async XLA Ops:
  0.6 76.2 %slice-start.2 = ((s8[7864320]{0:T(1024)(128)(4,1)}), s8[4194304]{0:T(1024)(128)(4,1)S(1)}, s32[]{:S(2)}) async-start(s8[7864320]{0:T(1024)(128)(4,1)} %bitcast.14), calls=%async_computation.2 | async-start | bytes 8388608
  1.8 19.1 %collective-permute-start.15 = (bf16[128,1280]{1,0:T(8,128)(2,1)S(1)}, bf16[128,1280]{1,0:T(8,128)(2,1)S(1)}, u32[]{:S(2)}, u32[]{:S(2)}) collective-permute-start(bf16[128,1280]{1,0:T(8,128)(2,1)S(1)} %slice_bitcast_fusion.refs_0_), channel_id=1, source_target_pairs={{0,2},{1,3},{2,0},{3,1},{4,6},{5,7},{6,4},{7,5},{8,10},{9,11},{10,... | collective-permute-start | bytes 983048 | tf_op jit(solution)/shard_map/ppermute | solution.py:205
  8.1 6.8 %collective-permute-start = (bf16[64,1280]{1,0:T(8,128)(2,1)S(1)}, bf16[64,1280]{1,0:T(8,128)(2,1)S(1)}, u32[]{:S(2)}, u32[]{:S(2)}) collective-permute-start(bf16[64,1280]{1,0:T(8,128)(2,1)S(1)} %get-tuple-element.49), channel_id=1, source_target_pairs={{0,8},{4,12},{8,0},{12,4},{16,24},{20,28},{24,16},{28,20},{1,9},{5... | collective-permute-start | bytes 491528 | tf_op jit(solution)/shard_map/ppermute | solution.py:66
  9.6 8.9 %collective-permute-start.1 = (bf16[64,1280]{1,0:T(8,128)(2,1)S(1)}, bf16[64,1280]{1,0:T(8,128)(2,1)S(1)}, u32[]{:S(2)}, u32[]{:S(2)}) collective-permute-start(bf16[64,1280]{1,0:T(8,128)(2,1)S(1)} %get-tuple-element.50), channel_id=1, source_target_pairs={{0,16},{4,20},{8,24},{12,28},{16,0},{20,4},{24,8},{28,12},{1,17},{... | collective-permute-start | bytes 491528 | tf_op jit(solution)/shard_map/ppermute | solution.py:66
  11.1 9.0 %collective-permute-start.2 = (bf16[64,1280]{1,0:T(8,128)(2,1)S(1)}, bf16[64,1280]{1,0:T(8,128)(2,1)S(1)}, u32[]{:S(2)}, u32[]{:S(2)}) collective-permute-start(bf16[64,1280]{1,0:T(8,128)(2,1)S(1)} %get-tuple-element.51), channel_id=1, source_target_pairs={{0,24},{4,28},{8,16},{12,20},{16,8},{20,12},{24,0},{28,4},{1,25},{... | collective-permute-start | bytes 491528 | tf_op jit(solution)/shard_map/ppermute | solution.py:66
  11.6 9.2 %collective-permute-start.3 = (bf16[64,1280]{1,0:T(8,128)(2,1)S(1)}, bf16[64,1280]{1,0:T(8,128)(2,1)S(1)}, u32[]{:S(2)}, u32[]{:S(2)}) collective-permute-start(bf16[64,1280]{1,0:T(8,128)(2,1)S(1)} %get-tuple-element.48.refs_0_), channel_id=1, source_target_pairs={{0,4},{4,0},{8,12},{12,8},{16,20},{20,16},{24,28},{28,24},{1,5},{5... | collective-permute-start | bytes 491528 | tf_op jit(solution)/shard_map/ppermute | solution.py:72
  14.9 7.3 %collective-permute-start.4 = (bf16[64,1280]{1,0:T(8,128)(2,1)S(1)}, bf16[64,1280]{1,0:T(8,128)(2,1)S(1)}, u32[]{:S(2)}, u32[]{:S(2)}) collective-permute-start(bf16[64,1280]{1,0:T(8,128)(2,1)S(1)} %collective-permute-done.refs_1_), channel_id=1, source_target_pairs={{0,4},{4,0},{8,12},{12,8},{16,20},{20,16},{24,28},{28,24},{1,5},{5... | collective-permute-start | bytes 491528 | tf_op jit(solution)/shard_map/ppermute | solution.py:72
  18.5 10.6 %collective-permute-start.14 = (bf16[128,1280]{1,0:T(8,128)(2,1)S(1)}, bf16[128,1280]{1,0:T(8,128)(2,1)S(1)}, u32[]{:S(2)}, u32[]{:S(2)}) collective-permute-start(bf16[128,1280]{1,0:T(8,128)(2,1)S(1)} %slice_bitcast_fusion.refs_0_), channel_id=1, source_target_pairs={{0,1},{1,0},{2,3},{3,2},{4,5},{5,4},{6,7},{7,6},{8,9},{9,8},{10,11... | collective-permute-start | bytes 983048 | tf_op jit(solution)/shard_map/ppermute | solution.py:205
  20.1 10.5 %collective-permute-start.16 = (bf16[128,1280]{1,0:T(8,128)(2,1)S(1)}, bf16[128,1280]{1,0:T(8,128)(2,1)S(1)}, u32[]{:S(2)}, u32[]{:S(2)}) collective-permute-start(bf16[128,1280]{1,0:T(8,128)(2,1)S(1)} %slice_bitcast_fusion.refs_0_), channel_id=1, source_target_pairs={{1,2},{2,1},{5,6},{6,5},{9,10},{10,9},{13,14},{14,13},{17,18},{18,... | collective-permute-start | bytes 983048 | tf_op jit(solution)/shard_map/ppermute | solution.py:205
  20.8 1.9 %collective-permute-start.5 = (bf16[64,1280]{1,0:T(8,128)(2,1)S(1)}, bf16[64,1280]{1,0:T(8,128)(2,1)S(1)}, u32[]{:S(2)}, u32[]{:S(2)}) collective-permute-start(bf16[64,1280]{1,0:T(8,128)(2,1)S(1)} %collective-permute-done.1.refs_2_), channel_id=1, source_target_pairs={{0,4},{4,0},{8,12},{12,8},{16,20},{20,16},{24,28},{28,24},{1,5},{5... | collective-permute-start | bytes 491528 | tf_op jit(solution)/shard_map/ppermute | solution.py:72
  20.9 13.8 %collective-permute-start.17 = (bf16[128,1280]{1,0:T(8,128)(2,1)S(1)}, bf16[128,1280]{1,0:T(8,128)(2,1)S(1)}, u32[]{:S(2)}, u32[]{:S(2)}) collective-permute-start(bf16[128,1280]{1,0:T(8,128)(2,1)S(1)} %collective-permute-done.15.refs_2_), channel_id=1, source_target_pairs={{1,0},{2,3},{5,4},{6,7},{9,8},{10,11},{13,12},{14,15},{17,16},{18,... | collective-permute-start | bytes 983048 | tf_op jit(solution)/shard_map/ppermute | solution.py:205
  22.2 1.6 %collective-permute-start.6 = (bf16[64,1280]{1,0:T(8,128)(2,1)S(1)}, bf16[64,1280]{1,0:T(8,128)(2,1)S(1)}, u32[]{:S(2)}, u32[]{:S(2)}) collective-permute-start(bf16[64,1280]{1,0:T(8,128)(2,1)S(1)} %collective-permute-done.2.refs_3_), channel_id=1, source_target_pairs={{0,4},{4,0},{8,12},{12,8},{16,20},{20,16},{24,28},{28,24},{1,5},{5... | collective-permute-start | bytes 491528 | tf_op jit(solution)/shard_map/ppermute | solution.py:72
  23.8 53.0 %slice-start = ((s8[7864320]{0:T(1024)(128)(4,1)}), s8[4194304]{0:T(1024)(128)(4,1)S(1)}, s32[]{:S(2)}) async-start(s8[7864320]{0:T(1024)(128)(4,1)} %bitcast.12), calls=%async_computation | async-start | bytes 8388608
  24.4 13.7 %collective-permute-start.7 = (bf16[64,1280]{1,0:T(8,128)(2,1)S(1)}, bf16[64,1280]{1,0:T(8,128)(2,1)S(1)}, u32[]{:S(2)}, u32[]{:S(2)}) collective-permute-start(bf16[64,1280]{1,0:T(8,128)(2,1)S(1)} %get-tuple-element.53), channel_id=1, source_target_pairs={{0,8},{4,12},{8,0},{12,4},{16,24},{20,28},{24,16},{28,20},{1,9},{5... | collective-permute-start | bytes 491528 | tf_op jit(solution)/shard_map/ppermute | solution.py:66
  25.8 12.8 %collective-permute-start.8 = (bf16[64,1280]{1,0:T(8,128)(2,1)S(1)}, bf16[64,1280]{1,0:T(8,128)(2,1)S(1)}, u32[]{:S(2)}, u32[]{:S(2)}) collective-permute-start(bf16[64,1280]{1,0:T(8,128)(2,1)S(1)} %get-tuple-element.54), channel_id=1, source_target_pairs={{0,16},{4,20},{8,24},{12,28},{16,0},{20,4},{24,8},{28,12},{1,17},{... | collective-permute-start | bytes 491528 | tf_op jit(solution)/shard_map/ppermute | solution.py:66
  29.1 47.7 %slice-start.3 = ((s8[7864320]{0:T(1024)(128)(4,1)}), s8[3670016]{0:T(1024)(128)(4,1)S(1)}, s32[]{:S(2)}) async-start(s8[7864320]{0:T(1024)(128)(4,1)} %bitcast.14), calls=%async_computation.3 | async-start | bytes 7340032
  29.1 9.6 %collective-permute-start.9 = (bf16[64,1280]{1,0:T(8,128)(2,1)S(1)}, bf16[64,1280]{1,0:T(8,128)(2,1)S(1)}, u32[]{:S(2)}, u32[]{:S(2)}) collective-permute-start(bf16[64,1280]{1,0:T(8,128)(2,1)S(1)} %get-tuple-element.55), channel_id=1, source_target_pairs={{0,24},{4,28},{8,16},{12,20},{16,8},{20,12},{24,0},{28,4},{1,25},{... | collective-permute-start | bytes 491528 | tf_op jit(solution)/shard_map/ppermute | solution.py:66
  35.0 10.7 %collective-permute-start.18 = (bf16[4,32,1280]{2,1,0:T(8,128)(2,1)S(1)}, bf16[4,32,1280]{2,1,0:T(8,128)(2,1)S(1)}, u32[]{:S(2)}, u32[]{:S(2)}) collective-permute-start(bf16[4,32,1280]{2,1,0:T(8,128)(2,1)S(1)} %get-tuple-element.59), channel_id=1, source_target_pairs={{0,8},{4,12},{8,0},{12,4},{16,24},{20,28},{24,16},{28,20},{1,9},{5... | collective-permute-start | bytes 983048 | tf_op jit(solution)/shard_map/ppermute | solution.py:66
  36.6 16.4 %collective-permute-start.19 = (bf16[4,32,1280]{2,1,0:T(8,128)(2,1)S(1)}, bf16[4,32,1280]{2,1,0:T(8,128)(2,1)S(1)}, u32[]{:S(2)}, u32[]{:S(2)}) collective-permute-start(bf16[4,32,1280]{2,1,0:T(8,128)(2,1)S(1)} %get-tuple-element.60), channel_id=1, source_target_pairs={{0,16},{4,20},{8,24},{12,28},{16,0},{20,4},{24,8},{28,12},{1,17},{... | collective-permute-start | bytes 983048 | tf_op jit(solution)/shard_map/ppermute | solution.py:66
  38.1 14.9 %collective-permute-start.20 = (bf16[4,32,1280]{2,1,0:T(8,128)(2,1)S(1)}, bf16[4,32,1280]{2,1,0:T(8,128)(2,1)S(1)}, u32[]{:S(2)}, u32[]{:S(2)}) collective-permute-start(bf16[4,32,1280]{2,1,0:T(8,128)(2,1)S(1)} %get-tuple-element.61), channel_id=1, source_target_pairs={{0,24},{4,28},{8,16},{12,20},{16,8},{20,12},{24,0},{28,4},{1,25},{... | collective-permute-start | bytes 983048 | tf_op jit(solution)/shard_map/ppermute | solution.py:66
  38.7 38.1 %slice-start.1 = ((s8[7864320]{0:T(1024)(128)(4,1)}), s8[3670016]{0:T(1024)(128)(4,1)S(1)}, s32[]{:S(2)}) async-start(s8[7864320]{0:T(1024)(128)(4,1)} %bitcast.12), calls=%async_computation.1 | async-start | bytes 7340032
  38.8 15.4 %collective-permute-start.11 = (bf16[104,1280]{1,0:T(8,128)(2,1)S(1)}, bf16[104,1280]{1,0:T(8,128)(2,1)S(1)}, u32[]{:S(2)}, u32[]{:S(2)}) collective-permute-start(bf16[104,1280]{1,0:T(8,128)(2,1)S(1)} %get-tuple-element.56.refs_9_), channel_id=1, source_target_pairs={{0,2},{1,3},{2,0},{3,1},{4,6},{5,7},{6,4},{7,5},{8,10},{9,11},{10,... | collective-permute-start | bytes 798728 | tf_op jit(solution)/shard_map/ppermute | solution.py:205
  40.5 13.8 %collective-permute-start.21 = (bf16[4,32,1280]{2,1,0:T(8,128)(2,1)S(1)}, bf16[4,32,1280]{2,1,0:T(8,128)(2,1)S(1)}, u32[]{:S(2)}, u32[]{:S(2)}) collective-permute-start(bf16[4,32,1280]{2,1,0:T(8,128)(2,1)S(1)} %get-tuple-element.58.refs_0_), channel_id=1, source_target_pairs={{0,4},{4,0},{8,12},{12,8},{16,20},{20,16},{24,28},{28,24},{1,5},{5... | collective-permute-start | bytes 983048 | tf_op jit(solution)/shard_map/ppermute | solution.py:72
  45.6 9.4 %collective-permute-start.22 = (bf16[4,32,1280]{2,1,0:T(8,128)(2,1)S(1)}, bf16[4,32,1280]{2,1,0:T(8,128)(2,1)S(1)}, u32[]{:S(2)}, u32[]{:S(2)}) collective-permute-start(bf16[4,32,1280]{2,1,0:T(8,128)(2,1)S(1)} %collective-permute-done.18.refs_1_), channel_id=1, source_target_pairs={{0,4},{4,0},{8,12},{12,8},{16,20},{20,16},{24,28},{28,24},{1,5},{5... | collective-permute-start | bytes 983048 | tf_op jit(solution)/shard_map/ppermute | solution.py:72
  53.0 3.4 %collective-permute-start.23 = (bf16[4,32,1280]{2,1,0:T(8,128)(2,1)S(1)}, bf16[4,32,1280]{2,1,0:T(8,128)(2,1)S(1)}, u32[]{:S(2)}, u32[]{:S(2)}) collective-permute-start(bf16[4,32,1280]{2,1,0:T(8,128)(2,1)S(1)} %collective-permute-done.19.refs_2_), channel_id=1, source_target_pairs={{0,4},{4,0},{8,12},{12,8},{16,20},{20,16},{24,28},{28,24},{1,5},{5... | collective-permute-start | bytes 983048 | tf_op jit(solution)/shard_map/ppermute | solution.py:72
  53.0 8.7 %collective-permute-start.24 = (bf16[4,32,1280]{2,1,0:T(8,128)(2,1)S(1)}, bf16[4,32,1280]{2,1,0:T(8,128)(2,1)S(1)}, u32[]{:S(2)}, u32[]{:S(2)}) collective-permute-start(bf16[4,32,1280]{2,1,0:T(8,128)(2,1)S(1)} %collective-permute-done.20.refs_3_), channel_id=1, source_target_pairs={{0,4},{4,0},{8,12},{12,8},{16,20},{20,16},{24,28},{28,24},{1,5},{5... | collective-permute-start | bytes 983048 | tf_op jit(solution)/shard_map/ppermute | solution.py:72
  54.2 9.1 %collective-permute-start.10 = (bf16[104,1280]{1,0:T(8,128)(2,1)S(1)}, bf16[104,1280]{1,0:T(8,128)(2,1)S(1)}, u32[]{:S(2)}, u32[]{:S(2)}) collective-permute-start(bf16[104,1280]{1,0:T(8,128)(2,1)S(1)} %get-tuple-element.56.refs_9_), channel_id=1, source_target_pairs={{0,1},{1,0},{2,3},{3,2},{4,5},{5,4},{6,7},{7,6},{8,9},{9,8},{10,11... | collective-permute-start | bytes 798728 | tf_op jit(solution)/shard_map/ppermute | solution.py:205
  54.3 10.3 %collective-permute-start.12 = (bf16[104,1280]{1,0:T(8,128)(2,1)S(1)}, bf16[104,1280]{1,0:T(8,128)(2,1)S(1)}, u32[]{:S(2)}, u32[]{:S(2)}) collective-permute-start(bf16[104,1280]{1,0:T(8,128)(2,1)S(1)} %get-tuple-element.56.refs_9_), channel_id=1, source_target_pairs={{1,2},{2,1},{5,6},{6,5},{9,10},{10,9},{13,14},{14,13},{17,18},{18,... | collective-permute-start | bytes 798728 | tf_op jit(solution)/shard_map/ppermute | solution.py:205
  55.0 13.3 %collective-permute-start.13 = (bf16[104,1280]{1,0:T(8,128)(2,1)S(1)}, bf16[104,1280]{1,0:T(8,128)(2,1)S(1)}, u32[]{:S(2)}, u32[]{:S(2)}) collective-permute-start(bf16[104,1280]{1,0:T(8,128)(2,1)S(1)} %collective-permute-done.11.refs_11_), channel_id=1, source_target_pairs={{1,0},{2,3},{5,4},{6,7},{9,8},{10,11},{13,12},{14,15},{17,16},{18,... | collective-permute-start | bytes 798728 | tf_op jit(solution)/shard_map/ppermute | solution.py:205
  56.4 20.4 %copy-start.2 = (f32[5120]{0:T(1024)S(1)}, f32[5120]{0:T(1024)}, u32[]{:S(2)}) copy-start(f32[5120]{0:T(1024)} %param.12) | copy-start | bytes 61444
  56.4 20.4 %copy-start.4 = (s32[8]{0:T(128)S(1)}, s32[8]{0:T(128)}, u32[]{:S(2)}) copy-start(s32[8]{0:T(128)} %refs_1_.5) | copy-start | bytes 100
  56.4 32.9 %collective-permute-start.29 = (bf16[128,1280]{1,0:T(8,128)(2,1)S(1)}, bf16[128,1280]{1,0:T(8,128)(2,1)S(1)}, u32[]{:S(2)}, u32[]{:S(2)}) collective-permute-start(bf16[128,1280]{1,0:T(8,128)(2,1)S(1)} %get-tuple-element.71.refs_9_), channel_id=1, source_target_pairs={{0,2},{1,3},{2,0},{3,1},{4,6},{5,7},{6,4},{7,5},{8,10},{9,11},{10,... | collective-permute-start | bytes 983048 | tf_op jit(solution)/shard_map/ppermute | solution.py:205
  62.5 27.5 %collective-permute-start.25 = (bf16[4,32,1280]{2,1,0:T(8,128)(2,1)S(1)}, bf16[4,32,1280]{2,1,0:T(8,128)(2,1)S(1)}, u32[]{:S(2)}, u32[]{:S(2)}) collective-permute-start(bf16[4,32,1280]{2,1,0:T(8,128)(2,1)S(1)} %get-tuple-element.63), channel_id=1, source_target_pairs={{0,8},{4,12},{8,0},{12,4},{16,24},{20,28},{24,16},{28,20},{1,9},{5... | collective-permute-start | bytes 983048 | tf_op jit(solution)/shard_map/ppermute | solution.py:66
  63.3 28.2 %collective-permute-start.26 = (bf16[4,32,1280]{2,1,0:T(8,128)(2,1)S(1)}, bf16[4,32,1280]{2,1,0:T(8,128)(2,1)S(1)}, u32[]{:S(2)}, u32[]{:S(2)}) collective-permute-start(bf16[4,32,1280]{2,1,0:T(8,128)(2,1)S(1)} %get-tuple-element.64), channel_id=1, source_target_pairs={{0,16},{4,20},{8,24},{12,28},{16,0},{20,4},{24,8},{28,12},{1,17},{... | collective-permute-start | bytes 983048 | tf_op jit(solution)/shard_map/ppermute | solution.py:66
  64.7 26.9 %collective-permute-start.27 = (bf16[4,32,1280]{2,1,0:T(8,128)(2,1)S(1)}, bf16[4,32,1280]{2,1,0:T(8,128)(2,1)S(1)}, u32[]{:S(2)}, u32[]{:S(2)}) collective-permute-start(bf16[4,32,1280]{2,1,0:T(8,128)(2,1)S(1)} %get-tuple-element.65), channel_id=1, source_target_pairs={{0,24},{4,28},{8,16},{12,20},{16,8},{20,12},{24,0},{28,4},{1,25},{... | collective-permute-start | bytes 983048 | tf_op jit(solution)/shard_map/ppermute | solution.py:66
  68.3 30.2 %collective-permute-start.28 = (bf16[128,1280]{1,0:T(8,128)(2,1)S(1)}, bf16[128,1280]{1,0:T(8,128)(2,1)S(1)}, u32[]{:S(2)}, u32[]{:S(2)}) collective-permute-start(bf16[128,1280]{1,0:T(8,128)(2,1)S(1)} %get-tuple-element.71.refs_9_), channel_id=1, source_target_pairs={{0,1},{1,0},{2,3},{3,2},{4,5},{5,4},{6,7},{7,6},{8,9},{9,8},{10,11... | collective-permute-start | bytes 983048 | tf_op jit(solution)/shard_map/ppermute | solution.py:205
  89.3 9.2 %collective-permute-start.30 = (bf16[128,1280]{1,0:T(8,128)(2,1)S(1)}, bf16[128,1280]{1,0:T(8,128)(2,1)S(1)}, u32[]{:S(2)}, u32[]{:S(2)}) collective-permute-start(bf16[128,1280]{1,0:T(8,128)(2,1)S(1)} %get-tuple-element.71.refs_9_), channel_id=1, source_target_pairs={{1,2},{2,1},{5,6},{6,5},{9,10},{10,9},{13,14},{14,13},{17,18},{18,... | collective-permute-start | bytes 983048 | tf_op jit(solution)/shard_map/ppermute | solution.py:205
  90.0 9.6 %collective-permute-start.31 = (bf16[128,1280]{1,0:T(8,128)(2,1)S(1)}, bf16[128,1280]{1,0:T(8,128)(2,1)S(1)}, u32[]{:S(2)}, u32[]{:S(2)}) collective-permute-start(bf16[128,1280]{1,0:T(8,128)(2,1)S(1)} %collective-permute-done.29.refs_11_), channel_id=1, source_target_pairs={{1,0},{2,3},{5,4},{6,7},{9,8},{10,11},{13,12},{14,15},{17,16},{18,... | collective-permute-start | bytes 983048 | tf_op jit(solution)/shard_map/ppermute | solution.py:205
  114.8 9.3 %collective-permute-start.34 = (bf16[104,1280]{1,0:T(8,128)(2,1)S(1)}, bf16[104,1280]{1,0:T(8,128)(2,1)S(1)}, u32[]{:S(2)}, u32[]{:S(2)}) collective-permute-start(bf16[104,1280]{1,0:T(8,128)(2,1)S(1)} %shard_map.124), channel_id=1, source_target_pairs={{0,1},{1,0},{2,3},{3,2},{4,5},{5,4},{6,7},{7,6},{8,9},{9,8},{10,11... | collective-permute-start | bytes 798728 | tf_op jit(solution)/shard_map/ppermute | solution.py:534
  117.0 20.0 %collective-permute-start.33 = (bf16[104,1280]{1,0:T(8,128)(2,1)S(1)}, bf16[104,1280]{1,0:T(8,128)(2,1)S(1)}, u32[]{:S(2)}, u32[]{:S(2)}) collective-permute-start(bf16[104,1280]{1,0:T(8,128)(2,1)S(1)} %shard_map.123), channel_id=1, source_target_pairs={{0,2},{1,3},{2,0},{3,1},{4,6},{5,7},{6,4},{7,5},{8,10},{9,11},{10,... | collective-permute-start | bytes 798728 | tf_op jit(solution)/shard_map/ppermute | solution.py:534
  117.8 19.2 %collective-permute-start.32 = (bf16[104,1280]{1,0:T(8,128)(2,1)S(1)}, bf16[104,1280]{1,0:T(8,128)(2,1)S(1)}, u32[]{:S(2)}, u32[]{:S(2)}) collective-permute-start(bf16[104,1280]{1,0:T(8,128)(2,1)S(1)} %shard_map.122), channel_id=1, source_target_pairs={{0,3},{1,2},{2,1},{3,0},{4,7},{5,6},{6,5},{7,4},{8,11},{9,10},{10,... | collective-permute-start | bytes 798728 | tf_op jit(solution)/shard_map/ppermute | solution.py:534
  137.2 4.5 %collective-permute-start.35 = (bf16[32,1280]{1,0:T(8,128)(2,1)S(1)}, bf16[32,1280]{1,0:T(8,128)(2,1)S(1)}, u32[]{:S(2)}, u32[]{:S(2)}) collective-permute-start(bf16[32,1280]{1,0:T(8,128)(2,1)S(1)} %get-tuple-element.85), channel_id=1, source_target_pairs={{0,8},{4,12},{8,0},{12,4},{16,24},{20,28},{24,16},{28,20},{1,9},{5... | collective-permute-start | bytes 245768 | tf_op jit(solution)/shard_map/ppermute | solution.py:66
  138.8 4.4 %collective-permute-start.36 = (bf16[32,1280]{1,0:T(8,128)(2,1)S(1)}, bf16[32,1280]{1,0:T(8,128)(2,1)S(1)}, u32[]{:S(2)}, u32[]{:S(2)}) collective-permute-start(bf16[32,1280]{1,0:T(8,128)(2,1)S(1)} %get-tuple-element.86), channel_id=1, source_target_pairs={{0,16},{4,20},{8,24},{12,28},{16,0},{20,4},{24,8},{28,12},{1,17},{... | collective-permute-start | bytes 245768 | tf_op jit(solution)/shard_map/ppermute | solution.py:66
  139.2 5.3 %collective-permute-start.37 = (bf16[32,1280]{1,0:T(8,128)(2,1)S(1)}, bf16[32,1280]{1,0:T(8,128)(2,1)S(1)}, u32[]{:S(2)}, u32[]{:S(2)}) collective-permute-start(bf16[32,1280]{1,0:T(8,128)(2,1)S(1)} %get-tuple-element.87), channel_id=1, source_target_pairs={{0,24},{4,28},{8,16},{12,20},{16,8},{20,12},{24,0},{28,4},{1,25},{... | collective-permute-start | bytes 245768 | tf_op jit(solution)/shard_map/ppermute | solution.py:66
  145.7 1.7 %collective-permute-start.38 = (bf16[4,32,1280]{2,1,0:T(8,128)(2,1)S(1)}, bf16[4,32,1280]{2,1,0:T(8,128)(2,1)S(1)}, u32[]{:S(2)}, u32[]{:S(2)}) collective-permute-start(bf16[4,32,1280]{2,1,0:T(8,128)(2,1)S(1)} %get-tuple-element.89), channel_id=1, source_target_pairs={{0,4},{4,0},{8,12},{12,8},{16,20},{20,16},{24,28},{28,24},{1,5},{5... | collective-permute-start | bytes 983048 | tf_op jit(solution)/shard_map/ppermute | solution.py:72
  147.4 4.6 %collective-permute-start.39 = (bf16[32,1280]{1,0:T(8,128)(2,1)S(1)}, bf16[32,1280]{1,0:T(8,128)(2,1)S(1)}, u32[]{:S(2)}, u32[]{:S(2)}) collective-permute-start(bf16[32,1280]{1,0:T(8,128)(2,1)S(1)} %get-tuple-element.91), channel_id=1, source_target_pairs={{0,8},{4,12},{8,0},{12,4},{16,24},{20,28},{24,16},{28,20},{1,9},{5... | collective-permute-start | bytes 245768 | tf_op jit(solution)/shard_map/ppermute | solution.py:66
  149.2 6.2 %collective-permute-start.40 = (bf16[32,1280]{1,0:T(8,128)(2,1)S(1)}, bf16[32,1280]{1,0:T(8,128)(2,1)S(1)}, u32[]{:S(2)}, u32[]{:S(2)}) collective-permute-start(bf16[32,1280]{1,0:T(8,128)(2,1)S(1)} %get-tuple-element.92), channel_id=1, source_target_pairs={{0,16},{4,20},{8,24},{12,28},{16,0},{20,4},{24,8},{28,12},{1,17},{... | collective-permute-start | bytes 245768 | tf_op jit(solution)/shard_map/ppermute | solution.py:66
  149.6 5.7 %collective-permute-start.41 = (bf16[32,1280]{1,0:T(8,128)(2,1)S(1)}, bf16[32,1280]{1,0:T(8,128)(2,1)S(1)}, u32[]{:S(2)}, u32[]{:S(2)}) collective-permute-start(bf16[32,1280]{1,0:T(8,128)(2,1)S(1)} %get-tuple-element.93), channel_id=1, source_target_pairs={{0,24},{4,28},{8,16},{12,20},{16,8},{20,12},{24,0},{28,4},{1,25},{... | collective-permute-start | bytes 245768 | tf_op jit(solution)/shard_map/ppermute | solution.py:66
  (7 other events, 58.0 us)
where the time goes:
time: 158 us; the launch traced here: 157 us
  starting transfers between devices  55.4 us (35%)
  waiting for transfers between devices  54.1 us (34%)
  Pallas kernels  36.5 us (23%)
  local copies, waits for them, and re-layouts  7.89 us (5%)
  other arithmetic  1.8 us (1%)
    pallas_call x17, Pallas kernels, call(): pl.pallas_call(body, out_shape=[jax.ShapeDtypeStruct(s, d) for s, d in ou...  36.5 us
    ppermute x12, starting transfers between devices, move(): return lax.ppermute(value, axis, pairs)  27.4 us
    ppermute x18, waiting for transfers between devices, to_groups(): got[k] = lax.ppermute(blocks[k], 'dp', group_pairs(count, k))  26.6 us
    ppermute x18, starting transfers between devices, to_groups(): got[k] = lax.ppermute(blocks[k], 'dp', group_pairs(count, k))  22.1 us
    ppermute x3, waiting for transfers between devices, on_device(): block = lax.ppermute(block, 'tensor', pairs)  15.8 us
    ppermute x12, waiting for transfers between devices, move(): return lax.ppermute(value, axis, pairs)  9.07 us
    unnamed x27, local copies, waits for them, and re-layouts  6.63 us
    ppermute x3, starting transfers between devices, on_device(): block = lax.ppermute(block, 'tensor', pairs)  4.67 us
  transfers between devices with their start and end apart: 42, of which 17 were waited for; matrix products, arithmetic and copies ran while one was open for 1% of the time, Pallas kernels for 13%

commit v1 on v0

--- a/solution.py
+++ b/solution.py
@@ -16,7 +16,7 @@
 ANY = pl.BlockSpec(memory_space=pl.ANY)
 PAIR = 2
 LIMIT = 16 << 20
-WAIT = 10**9
+WAIT = 2 * 10**9
 
 
 def up_to(value, step):
@@ -369,6 +369,14 @@
     gn = gn + jnp.dot(wv[at, :], turned[1], preferred_element_type=F32)
     gn = gn.T[:lead] * gain[to]
     out[...] = (inv_lead[:, :1] * gn - x_lead[to].astype(F32) * pull[:, :1]).astype(BF16)
+
+
+def stack_body(lead_rows, *refs):
+    out, at = refs[-1], 0
+    for i, part in enumerate(refs[:-1]):
+        n = part.shape[0] if i else lead_rows
+        out[0, at : at + n, :] = part[:n, :]
+        at += n
 
 
 def sum_body(count, n, *refs):
@@ -518,7 +526,6 @@
             if first:
                 saved = list(got[5:])
         start += rows
-    output = jnp.concatenate([outputs[0][:prompt_len], *outputs[1:]], axis=0)[None]
 
     x_lead, inv_lead, _, _, turned_q = saved
     got = []
@@ -533,6 +540,12 @@
             pairs = [(i, i ^ k if tp & (tp - 1) == 0 else (i + k) % tp) for i in range(tp)]
             block = lax.ppermute(block, "tensor", pairs)
         got.append(block)
+    (output,) = call(
+        functools.partial(stack_body, prompt_len),
+        [((1, prompt_len + text_len, cols), BF16)],
+        [VM] * len(outputs),
+        outputs,
+    )
     pieces = call(
         functools.partial(sum_body, count, tp),
         [((prompt_q, width), BF16)] * count,

time: 158 us -> 155 us (0.981)
  local copies, waits for them, and re-layouts: 7.89 us -> 4.58 us
  starting transfers between devices: 55.4 us -> 53.3 us
  waiting for transfers between devices: 54.1 us -> 56.2 us
    unnamed x27, local copies, waits for them, and re-layouts: 6.63 us -> 3.41 us
    ppermute x12, waiting for transfers between devices: 9.07 us -> 11.9 us  [move(): return lax.ppermute(value, axis, pairs)]
    ppermute x12, starting transfers between devices: 27.4 us -> 25.6 us  [move(): return lax.ppermute(value, axis, pairs)]
    pallas_call x17 -> x18, Pallas kernels: 36.5 us -> 37.9 us  [call(): pl.pallas_call(body, out_shape=[jax.ShapeDtypeStruct(s, d) for s, d in ou...]
  transfers between devices with their start and end apart: 42 -> 42, of which waited for: 17 -> 16; matrix products, arithmetic and copies ran while one was open for 1% -> 1% of each run, Pallas kernels for 13% -> 14%
where the time goes in v1:
time: 155 us; the launch traced here: 154 us
  waiting for transfers between devices  56.2 us (36%)
  starting transfers between devices  53.3 us (34%)
  Pallas kernels  37.9 us (24%)
  local copies, waits for them, and re-layouts  4.58 us (3%)
    pallas_call x18, Pallas kernels, call(): pl.pallas_call(body, out_shape=[jax.ShapeDtypeStruct(s, d) for s, d in ou...  37.9 us
    ppermute x18, waiting for transfers between devices, to_groups(): got[k] = lax.ppermute(blocks[k], 'dp', group_pairs(count, k))  26.7 us
    ppermute x12, starting transfers between devices, move(): return lax.ppermute(value, axis, pairs)  25.6 us
    ppermute x18, starting transfers between devices, to_groups(): got[k] = lax.ppermute(blocks[k], 'dp', group_pairs(count, k))  21.8 us
    ppermute x3, waiting for transfers between devices, on_device(): block = lax.ppermute(block, 'tensor', pairs)  15.9 us
    ppermute x12, waiting for transfers between devices, move(): return lax.ppermute(value, axis, pairs)  11.9 us
    ppermute x3, starting transfers between devices, on_device(): block = lax.ppermute(block, 'tensor', pairs)  4.77 us
    unnamed x27, local copies, waits for them, and re-layouts  3.41 us
  transfers between devices with their start and end apart: 42, of which 16 were waited for; matrix products, arithmetic and copies ran while one was open for 1% of the time, Pallas kernels for 14%

profile of v1, /device:TPU:0, one launch (start us, length us, event | category | flops | bytes accessed | tf_op | source)
XLA Modules:
  0.0 154.0 jit_solution(4741579579119003603)
XLA Ops:
  0.7 1.1 slice_bitcast_fusion.refs_0_
  1.7 4.1 %collective-permute-start.15 = (bf16[128,1280]{1,0:T(8,128)(2,1)S(1)}, bf16[128,1280]{1,0:T(8,128)(2,1)S(1)}, u32[]{:S(2)}, u32[]{:S(2)}) collective-permute-start(bf16[128,1280]{1,0:T(8,128)(2,1)S(1)} %slice_bitcast_fusion.refs_0_), channel_id=1, source_target_pairs={{0,2},{1,3},{2,0},{3,1},{4,6},{5,7},{6,4},{7,5},{8,10},{9,11},{10,... | collective-permute-start | bytes 983048 | tf_op jit(solution)/shard_map/ppermute | solution.py:205
  5.8 1.1 copy-done.1
  8.0 1.6 %collective-permute-start = (bf16[64,1280]{1,0:T(8,128)(2,1)S(1)}, bf16[64,1280]{1,0:T(8,128)(2,1)S(1)}, u32[]{:S(2)}, u32[]{:S(2)}) collective-permute-start(bf16[64,1280]{1,0:T(8,128)(2,1)S(1)} %get-tuple-element.49), channel_id=1, source_target_pairs={{0,8},{4,12},{8,0},{12,4},{16,24},{20,28},{24,16},{28,20},{1,9},{5... | collective-permute-start | bytes 491528 | tf_op jit(solution)/shard_map/ppermute | solution.py:66
  9.5 1.5 collective-permute-start.1
  11.5 3.3 %collective-permute-done.refs_1_ = bf16[64,1280]{1,0:T(8,128)(2,1)S(1)} collective-permute-done((bf16[64,1280]{1,0:T(8,128)(2,1)S(1)}, bf16[64,1280]{1,0:T(8,128)(2,1)S(1)}, u32[]{:S(2)}, u32[]{:S(2)}) %collective-permute-start) | collective-permute-done | bytes 163872 | tf_op jit(solution)/shard_map/ppermute | solution.py:66
  14.8 3.6 %collective-permute-done.1.refs_2_ = bf16[64,1280]{1,0:T(8,128)(2,1)S(1)} collective-permute-done((bf16[64,1280]{1,0:T(8,128)(2,1)S(1)}, bf16[64,1280]{1,0:T(8,128)(2,1)S(1)}, u32[]{:S(2)}, u32[]{:S(2)}) %collective-permute-start.1) | collective-permute-done | bytes 163872 | tf_op jit(solution)/shard_map/ppermute | solution.py:66
  18.4 1.6 %collective-permute-start.14 = (bf16[128,1280]{1,0:T(8,128)(2,1)S(1)}, bf16[128,1280]{1,0:T(8,128)(2,1)S(1)}, u32[]{:S(2)}, u32[]{:S(2)}) collective-permute-start(bf16[128,1280]{1,0:T(8,128)(2,1)S(1)} %slice_bitcast_fusion.refs_0_), channel_id=1, source_target_pairs={{0,1},{1,0},{2,3},{3,2},{4,5},{5,4},{6,7},{7,6},{8,9},{9,8},{10,11... | collective-permute-start | bytes 983048 | tf_op jit(solution)/shard_map/ppermute | solution.py:205
  21.3 1.3 collective-permute-start.17
  23.4 1.0 collective-permute-start.7
  24.4 1.5 collective-permute-start.8
  26.0 3.1 %collective-permute-done.14.refs_1_ = bf16[128,1280]{1,0:T(8,128)(2,1)S(1)} collective-permute-done((bf16[128,1280]{1,0:T(8,128)(2,1)S(1)}, bf16[128,1280]{1,0:T(8,128)(2,1)S(1)}, u32[]{:S(2)}, u32[]{:S(2)}) %collective-permute-start.14) | collective-permute-done | bytes 327712 | tf_op jit(solution)/shard_map/ppermute | solution.py:205
  29.0 1.5 collective-permute-start.9
  30.5 4.1 %collective-permute-done.17.refs_4_ = bf16[128,1280]{1,0:T(8,128)(2,1)S(1)} collective-permute-done((bf16[128,1280]{1,0:T(8,128)(2,1)S(1)}, bf16[128,1280]{1,0:T(8,128)(2,1)S(1)}, u32[]{:S(2)}, u32[]{:S(2)}) %collective-permute-start.17) | collective-permute-done | bytes 327712 | tf_op jit(solution)/shard_map/ppermute | solution.py:205
  34.9 1.6 %collective-permute-start.18 = (bf16[4,32,1280]{2,1,0:T(8,128)(2,1)S(1)}, bf16[4,32,1280]{2,1,0:T(8,128)(2,1)S(1)}, u32[]{:S(2)}, u32[]{:S(2)}) collective-permute-start(bf16[4,32,1280]{2,1,0:T(8,128)(2,1)S(1)} %get-tuple-element.59), channel_id=1, source_target_pairs={{0,8},{4,12},{8,0},{12,4},{16,24},{20,28},{24,16},{28,20},{1,9},{5... | collective-permute-start | bytes 983048 | tf_op jit(solution)/shard_map/ppermute | solution.py:66
  36.5 1.5 collective-permute-start.19
  38.7 1.7 %collective-permute-start.11 = (bf16[104,1280]{1,0:T(8,128)(2,1)S(1)}, bf16[104,1280]{1,0:T(8,128)(2,1)S(1)}, u32[]{:S(2)}, u32[]{:S(2)}) collective-permute-start(bf16[104,1280]{1,0:T(8,128)(2,1)S(1)} %get-tuple-element.56.refs_9_), channel_id=1, source_target_pairs={{0,2},{1,3},{2,0},{3,1},{4,6},{5,7},{6,4},{7,5},{8,10},{9,11},{10,... | collective-permute-start | bytes 798728 | tf_op jit(solution)/shard_map/ppermute | solution.py:205
  40.3 5.2 %collective-permute-done.18.refs_1_ = bf16[4,32,1280]{2,1,0:T(8,128)(2,1)S(1)} collective-permute-done((bf16[4,32,1280]{2,1,0:T(8,128)(2,1)S(1)}, bf16[4,32,1280]{2,1,0:T(8,128)(2,1)S(1)}, u32[]{:S(2)}, u32[]{:S(2)}) %collective-permute-start.18) | collective-permute-done | bytes 327712 | tf_op jit(solution)/shard_map/ppermute | solution.py:66
  45.6 7.3 %collective-permute-done.19.refs_2_ = bf16[4,32,1280]{2,1,0:T(8,128)(2,1)S(1)} collective-permute-done((bf16[4,32,1280]{2,1,0:T(8,128)(2,1)S(1)}, bf16[4,32,1280]{2,1,0:T(8,128)(2,1)S(1)}, u32[]{:S(2)}, u32[]{:S(2)}) %collective-permute-start.19) | collective-permute-done | bytes 327712 | tf_op jit(solution)/shard_map/ppermute | solution.py:66
  55.0 5.3 %collective-permute-start.29 = (bf16[128,1280]{1,0:T(8,128)(2,1)S(1)}, bf16[128,1280]{1,0:T(8,128)(2,1)S(1)}, u32[]{:S(2)}, u32[]{:S(2)}) collective-permute-start(bf16[128,1280]{1,0:T(8,128)(2,1)S(1)} %get-tuple-element.71.refs_9_), channel_id=1, source_target_pairs={{0,2},{1,3},{2,0},{3,1},{4,6},{5,7},{6,4},{7,5},{8,10},{9,11},{10,... | collective-permute-start | bytes 983048 | tf_op jit(solution)/shard_map/ppermute | solution.py:205
  60.3 1.3 collective-permute-start.13
  63.2 1.3 collective-permute-start.26
  64.5 1.4 collective-permute-start.27
  66.2 3.8 %collective-permute-done.13.refs_13_ = bf16[104,1280]{1,0:T(8,128)(2,1)S(1)} collective-permute-done((bf16[104,1280]{1,0:T(8,128)(2,1)S(1)}, bf16[104,1280]{1,0:T(8,128)(2,1)S(1)}, u32[]{:S(2)}, u32[]{:S(2)}) %collective-permute-start.13) | collective-permute-done | bytes 266272 | tf_op jit(solution)/shard_map/ppermute | solution.py:205
  69.9 6.8 %collective-permute-start.28 = (bf16[128,1280]{1,0:T(8,128)(2,1)S(1)}, bf16[128,1280]{1,0:T(8,128)(2,1)S(1)}, u32[]{:S(2)}, u32[]{:S(2)}) collective-permute-start(bf16[128,1280]{1,0:T(8,128)(2,1)S(1)} %get-tuple-element.71.refs_9_), channel_id=1, source_target_pairs={{0,1},{1,0},{2,3},{3,2},{4,5},{5,4},{6,7},{7,6},{8,9},{9,8},{10,11... | collective-permute-start | bytes 983048 | tf_op jit(solution)/shard_map/ppermute | solution.py:205
  76.8 9.4 %shard_map.116 = (bf16[104,768]{1,0:T(8,128)(2,1)S(1)}, bf16[104,768]{1,0:T(8,128)(2,1)S(1)}, bf16[104,768]{1,0:T(8,128)(2,1)S(1)}, f32[128,768]{1,0:T(8,128)S(1...) custom-call(s32[8]{0:T(128)S(1)} %copy-done.3, ...), custom_call_target="tpu_custom_call" | custom-call | flops 2453667840 | bytes 1048576 | tf_op jit(solution)/shard_map/pallas_call | solution.py:27
  86.9 1.5 collective-permute-start.31
  88.6 6.9 %shard_map.120 = (bf16[128,768]{1,0:T(8,128)(2,1)S(1)}, bf16[128,768]{1,0:T(8,128)(2,1)S(1)}, bf16[128,768]{1,0:T(8,128)(2,1)S(1)}, f32[128,768]{1,0:T(8,128)S(1)}, f32[128,768]{1,0:T(8,128)S(1)}) custom-call(s32[8]{0:T(128)S(1)} %copy-done.3, s32[8]{0:T(128)S(1)} %copy-done.2, f32[4,1,1280]{2,1,0:T(1,128)S(1)} %bitcast.16, bf16[5120,768]{1,0:T(8,128)(2,1)S(1)} %bitcast.10, ...), custom_call_target="tpu_custom_call" | custom-call | flops 3019898880 | bytes 1048576 | tf_op jit(solution)/shard_map/pallas_call | solution.py:27
  95.5 1.0 collective-permute-done.31.refs_13_
  96.5 9.9 %shard_map.121 = (bf16[128,768]{1,0:T(8,128)(2,1)S(1)}, bf16[2,768,128]{2,1,0:T(8,128)(2,1)S(1)}, f32[104,128]{1,0:T(8,128)S(1)}) custom-call(s32[8]{0:T(128)S(1)} %copy-done.3, s32[8]{0:T(128)S(1)} %copy-done.2, f32[4,1,1280]{2,1,0:T(1,128)S(1)} %bitcast.17, bf16[5120,768]{1,0:T(8,128)(2,1)S(1)} %bitcast.10, bf16[5120,768]{1,0:T(8,128)(2,1)S(1)} %bitcast.12, ...), custom_call_target="tpu_custom_call" | custom-call | flops 3019898880 | bytes 1048576 | tf_op jit(solution)/shard_map/pallas_call | solution.py:27
  106.4 1.8 %shard_map.125 = bf16[104,1280]{1,0:T(8,128)(2,1)S(1)} custom-call(f32[4,1,1280]{2,1,0:T(1,128)S(1)} %bitcast.18, bf16[5120,768]{1,0:T(8,128)(2,1)S(1)} %bitcast.10, bf16[5120,768]{1,0:T(8,128)(2,1)S(1)} %bitcast.12, bf16[5120,768]{1,0:T(8,128)(2,1)S(1)} %bitcast.14, bf16[4,104,1280]{2,1,0:T(8,128)(2,1)S(1)} %get-tuple-element.80.x_lead, ...), custom_call_target="tpu_custom_call" | custom-call | flops 2000000000 | bytes 1048576 | tf_op jit(solution)/shard_map/pallas_call | solution.py:27
  108.2 1.8 %shard_map.124 = bf16[104,1280]{1,0:T(8,128)(2,1)S(1)} custom-call(f32[4,1,1280]{2,1,0:T(1,128)S(1)} %bitcast.19, bf16[5120,768]{1,0:T(8,128)(2,1)S(1)} %bitcast.10, bf16[5120,768]{1,0:T(8,128)(2,1)S(1)} %bitcast.12, bf16[5120,768]{1,0:T(8,128)(2,1)S(1)} %bitcast.14, bf16[4,104,1280]{2,1,0:T(8,128)(2,1)S(1)} %get-tuple-element.80.x_lead, ...), custom_call_target="tpu_custom_call" | custom-call | flops 2000000000 | bytes 1048576 | tf_op jit(solution)/shard_map/pallas_call | solution.py:27
  110.0 1.8 %shard_map.123 = bf16[104,1280]{1,0:T(8,128)(2,1)S(1)} custom-call(f32[4,1,1280]{2,1,0:T(1,128)S(1)} %bitcast.20, bf16[5120,768]{1,0:T(8,128)(2,1)S(1)} %bitcast.10, bf16[5120,768]{1,0:T(8,128)(2,1)S(1)} %bitcast.12, bf16[5120,768]{1,0:T(8,128)(2,1)S(1)} %bitcast.14, bf16[4,104,1280]{2,1,0:T(8,128)(2,1)S(1)} %get-tuple-element.80.x_lead, ...), custom_call_target="tpu_custom_call" | custom-call | flops 2000000000 | bytes 1048576 | tf_op jit(solution)/shard_map/pallas_call | solution.py:27
  111.8 2.3 %collective-permute-start.34 = (bf16[104,1280]{1,0:T(8,128)(2,1)S(1)}, bf16[104,1280]{1,0:T(8,128)(2,1)S(1)}, u32[]{:S(2)}, u32[]{:S(2)}) collective-permute-start(bf16[104,1280]{1,0:T(8,128)(2,1)S(1)} %shard_map.125), channel_id=1, source_target_pairs={{0,1},{1,0},{2,3},{3,2},{4,5},{5,4},{6,7},{7,6},{8,9},{9,8},{10,11... | collective-permute-start | bytes 798728 | tf_op jit(solution)/shard_map/ppermute | solution.py:541
  115.0 1.6 %collective-permute-start.32 = (bf16[104,1280]{1,0:T(8,128)(2,1)S(1)}, bf16[104,1280]{1,0:T(8,128)(2,1)S(1)}, u32[]{:S(2)}, u32[]{:S(2)}) collective-permute-start(bf16[104,1280]{1,0:T(8,128)(2,1)S(1)} %shard_map.123), channel_id=1, source_target_pairs={{0,3},{1,2},{2,1},{3,0},{4,7},{5,6},{6,5},{7,4},{8,11},{9,10},{10,... | collective-permute-start | bytes 798728 | tf_op jit(solution)/shard_map/ppermute | solution.py:541
  116.5 1.8 %shard_map.126.refs_3_ = bf16[104,1280]{1,0:T(8,128)(2,1)S(1)} custom-call(f32[4,1,1280]{2,1,0:T(1,128)S(1)} %bitcast.21, bf16[5120,768]{1,0:T(8,128)(2,1)S(1)} %bitcast.10, bf16[5120,768]{1,0:T(8,128)(2,1)S(1)} %bitcast.12, bf16[5120,768]{1,0:T(8,128)(2,1)S(1)} %bitcast.14, bf16[4,104,1280]{2,1,0:T(8,128)(2,1)S(1)} %get-tuple-element.80.x_lead, ...), custom_call_target="tpu_custom_call" | custom-call | flops 2000000000 | bytes 1048576 | tf_op jit(solution)/shard_map/pallas_call | solution.py:27
  118.3 3.1 %collective-permute-done.34.refs_2_ = bf16[104,1280]{1,0:T(8,128)(2,1)S(1)} collective-permute-done((bf16[104,1280]{1,0:T(8,128)(2,1)S(1)}, bf16[104,1280]{1,0:T(8,128)(2,1)S(1)}, u32[]{:S(2)}, u32[]{:S(2)}) %collective-permute-start.34) | collective-permute-done | bytes 266272 | tf_op jit(solution)/shard_map/ppermute | solution.py:541
  121.5 12.8 %collective-permute-done.33.refs_1_ = bf16[104,1280]{1,0:T(8,128)(2,1)S(1)} collective-permute-done((bf16[104,1280]{1,0:T(8,128)(2,1)S(1)}, bf16[104,1280]{1,0:T(8,128)(2,1)S(1)}, u32[]{:S(2)}, u32[]{:S(2)}) %collective-permute-start.33) | collective-permute-done | bytes 266272 | tf_op jit(solution)/shard_map/ppermute | solution.py:541
  134.5 1.6 %collective-permute-start.35 = (bf16[32,1280]{1,0:T(8,128)(2,1)S(1)}, bf16[32,1280]{1,0:T(8,128)(2,1)S(1)}, u32[]{:S(2)}, u32[]{:S(2)}) collective-permute-start(bf16[32,1280]{1,0:T(8,128)(2,1)S(1)} %get-tuple-element.85), channel_id=1, source_target_pairs={{0,8},{4,12},{8,0},{12,4},{16,24},{20,28},{24,16},{28,20},{1,9},{5... | collective-permute-start | bytes 245768 | tf_op jit(solution)/shard_map/ppermute | solution.py:66
  136.5 1.5 collective-permute-start.37
  139.0 1.5 collective-permute-done.36.refs_2_
  140.5 1.4 collective-permute-done.37.refs_3_
  141.9 1.1 shard_map.128
  143.0 1.6 %collective-permute-done.38.other = bf16[4,32,1280]{2,1,0:T(8,128)(2,1)S(1)} collective-permute-done((bf16[4,32,1280]{2,1,0:T(8,128)(2,1)S(1)}, bf16[4,32,1280]{2,1,0:T(8,128)(2,1)S(1)}, u32[]{:S(2)}, u32[]{:S(2)}) %collective-permute-start.38) | collective-permute-done | bytes 327712 | tf_op jit(solution)/shard_map/ppermute | solution.py:72
  144.7 1.7 %collective-permute-start.39 = (bf16[32,1280]{1,0:T(8,128)(2,1)S(1)}, bf16[32,1280]{1,0:T(8,128)(2,1)S(1)}, u32[]{:S(2)}, u32[]{:S(2)}) collective-permute-start(bf16[32,1280]{1,0:T(8,128)(2,1)S(1)} %get-tuple-element.91), channel_id=1, source_target_pairs={{0,8},{4,12},{8,0},{12,4},{16,24},{20,28},{24,16},{28,20},{1,9},{5... | collective-permute-start | bytes 245768 | tf_op jit(solution)/shard_map/ppermute | solution.py:66
  146.9 1.4 collective-permute-start.41
  149.3 3.3 %collective-permute-done.40.refs_2_ = bf16[32,1280]{1,0:T(8,128)(2,1)S(1)} collective-permute-done((bf16[32,1280]{1,0:T(8,128)(2,1)S(1)}, bf16[32,1280]{1,0:T(8,128)(2,1)S(1)}, u32[]{:S(2)}, u32[]{:S(2)}) %collective-permute-start.40) | collective-permute-done | bytes 81952 | tf_op jit(solution)/shard_map/ppermute | solution.py:66
  152.7 1.3 copy.12
  (92 shorter events, 13.4 us)
Async XLA Ops:
  1.7 19.1 %collective-permute-start.15 = (bf16[128,1280]{1,0:T(8,128)(2,1)S(1)}, bf16[128,1280]{1,0:T(8,128)(2,1)S(1)}, u32[]{:S(2)}, u32[]{:S(2)}) collective-permute-start(bf16[128,1280]{1,0:T(8,128)(2,1)S(1)} %slice_bitcast_fusion.refs_0_), channel_id=1, source_target_pairs={{0,2},{1,3},{2,0},{3,1},{4,6},{5,7},{6,4},{7,5},{8,10},{9,11},{10,... | collective-permute-start | bytes 983048 | tf_op jit(solution)/shard_map/ppermute | solution.py:205
  7.9 68.8 %slice-start.4 = ((s8[7864320]{0:T(1024)(128)(4,1)}), s8[4194304]{0:T(1024)(128)(4,1)S(1)}, s32[]{:S(2)}) async-start(s8[7864320]{0:T(1024)(128)(4,1)} %bitcast.13), calls=%async_computation.4 | async-start | bytes 8388608
  8.0 6.8 %collective-permute-start = (bf16[64,1280]{1,0:T(8,128)(2,1)S(1)}, bf16[64,1280]{1,0:T(8,128)(2,1)S(1)}, u32[]{:S(2)}, u32[]{:S(2)}) collective-permute-start(bf16[64,1280]{1,0:T(8,128)(2,1)S(1)} %get-tuple-element.49), channel_id=1, source_target_pairs={{0,8},{4,12},{8,0},{12,4},{16,24},{20,28},{24,16},{28,20},{1,9},{5... | collective-permute-start | bytes 491528 | tf_op jit(solution)/shard_map/ppermute | solution.py:66
  9.5 8.9 %collective-permute-start.1 = (bf16[64,1280]{1,0:T(8,128)(2,1)S(1)}, bf16[64,1280]{1,0:T(8,128)(2,1)S(1)}, u32[]{:S(2)}, u32[]{:S(2)}) collective-permute-start(bf16[64,1280]{1,0:T(8,128)(2,1)S(1)} %get-tuple-element.50), channel_id=1, source_target_pairs={{0,16},{4,20},{8,24},{12,28},{16,0},{20,4},{24,8},{28,12},{1,17},{... | collective-permute-start | bytes 491528 | tf_op jit(solution)/shard_map/ppermute | solution.py:66
  11.1 9.0 %collective-permute-start.2 = (bf16[64,1280]{1,0:T(8,128)(2,1)S(1)}, bf16[64,1280]{1,0:T(8,128)(2,1)S(1)}, u32[]{:S(2)}, u32[]{:S(2)}) collective-permute-start(bf16[64,1280]{1,0:T(8,128)(2,1)S(1)} %get-tuple-element.51), channel_id=1, source_target_pairs={{0,24},{4,28},{8,16},{12,20},{16,8},{20,12},{24,0},{28,4},{1,25},{... | collective-permute-start | bytes 491528 | tf_op jit(solution)/shard_map/ppermute | solution.py:66
  11.5 9.2 %collective-permute-start.3 = (bf16[64,1280]{1,0:T(8,128)(2,1)S(1)}, bf16[64,1280]{1,0:T(8,128)(2,1)S(1)}, u32[]{:S(2)}, u32[]{:S(2)}) collective-permute-start(bf16[64,1280]{1,0:T(8,128)(2,1)S(1)} %get-tuple-element.48.refs_0_), channel_id=1, source_target_pairs={{0,4},{4,0},{8,12},{12,8},{16,20},{20,16},{24,28},{28,24},{1,5},{5... | collective-permute-start | bytes 491528 | tf_op jit(solution)/shard_map/ppermute | solution.py:72
  14.8 6.5 %collective-permute-start.4 = (bf16[64,1280]{1,0:T(8,128)(2,1)S(1)}, bf16[64,1280]{1,0:T(8,128)(2,1)S(1)}, u32[]{:S(2)}, u32[]{:S(2)}) collective-permute-start(bf16[64,1280]{1,0:T(8,128)(2,1)S(1)} %collective-permute-done.refs_1_), channel_id=1, source_target_pairs={{0,4},{4,0},{8,12},{12,8},{16,20},{20,16},{24,28},{28,24},{1,5},{5... | collective-permute-start | bytes 491528 | tf_op jit(solution)/shard_map/ppermute | solution.py:72
  18.4 10.6 %collective-permute-start.14 = (bf16[128,1280]{1,0:T(8,128)(2,1)S(1)}, bf16[128,1280]{1,0:T(8,128)(2,1)S(1)}, u32[]{:S(2)}, u32[]{:S(2)}) collective-permute-start(bf16[128,1280]{1,0:T(8,128)(2,1)S(1)} %slice_bitcast_fusion.refs_0_), channel_id=1, source_target_pairs={{0,1},{1,0},{2,3},{3,2},{4,5},{5,4},{6,7},{7,6},{8,9},{9,8},{10,11... | collective-permute-start | bytes 983048 | tf_op jit(solution)/shard_map/ppermute | solution.py:205
  20.0 10.5 %collective-permute-start.16 = (bf16[128,1280]{1,0:T(8,128)(2,1)S(1)}, bf16[128,1280]{1,0:T(8,128)(2,1)S(1)}, u32[]{:S(2)}, u32[]{:S(2)}) collective-permute-start(bf16[128,1280]{1,0:T(8,128)(2,1)S(1)} %slice_bitcast_fusion.refs_0_), channel_id=1, source_target_pairs={{1,2},{2,1},{5,6},{6,5},{9,10},{10,9},{13,14},{14,13},{17,18},{18,... | collective-permute-start | bytes 983048 | tf_op jit(solution)/shard_map/ppermute | solution.py:205
  20.7 2.0 %collective-permute-start.5 = (bf16[64,1280]{1,0:T(8,128)(2,1)S(1)}, bf16[64,1280]{1,0:T(8,128)(2,1)S(1)}, u32[]{:S(2)}, u32[]{:S(2)}) collective-permute-start(bf16[64,1280]{1,0:T(8,128)(2,1)S(1)} %collective-permute-done.1.refs_2_), channel_id=1, source_target_pairs={{0,4},{4,0},{8,12},{12,8},{16,20},{20,16},{24,28},{28,24},{1,5},{5... | collective-permute-start | bytes 491528 | tf_op jit(solution)/shard_map/ppermute | solution.py:72
  20.8 1.9 %collective-permute-start.6 = (bf16[64,1280]{1,0:T(8,128)(2,1)S(1)}, bf16[64,1280]{1,0:T(8,128)(2,1)S(1)}, u32[]{:S(2)}, u32[]{:S(2)}) collective-permute-start(bf16[64,1280]{1,0:T(8,128)(2,1)S(1)} %collective-permute-done.2.refs_3_), channel_id=1, source_target_pairs={{0,4},{4,0},{8,12},{12,8},{16,20},{20,16},{24,28},{28,24},{1,5},{5... | collective-permute-start | bytes 491528 | tf_op jit(solution)/shard_map/ppermute | solution.py:72
  21.3 13.3 %collective-permute-start.17 = (bf16[128,1280]{1,0:T(8,128)(2,1)S(1)}, bf16[128,1280]{1,0:T(8,128)(2,1)S(1)}, u32[]{:S(2)}, u32[]{:S(2)}) collective-permute-start(bf16[128,1280]{1,0:T(8,128)(2,1)S(1)} %collective-permute-done.15.refs_2_), channel_id=1, source_target_pairs={{1,0},{2,3},{5,4},{6,7},{9,8},{10,11},{13,12},{14,15},{17,16},{18,... | collective-permute-start | bytes 983048 | tf_op jit(solution)/shard_map/ppermute | solution.py:205
  23.4 14.6 %collective-permute-start.7 = (bf16[64,1280]{1,0:T(8,128)(2,1)S(1)}, bf16[64,1280]{1,0:T(8,128)(2,1)S(1)}, u32[]{:S(2)}, u32[]{:S(2)}) collective-permute-start(bf16[64,1280]{1,0:T(8,128)(2,1)S(1)} %get-tuple-element.53), channel_id=1, source_target_pairs={{0,8},{4,12},{8,0},{12,4},{16,24},{20,28},{24,16},{28,20},{1,9},{5... | collective-permute-start | bytes 491528 | tf_op jit(solution)/shard_map/ppermute | solution.py:66
  24.4 14.1 %collective-permute-start.8 = (bf16[64,1280]{1,0:T(8,128)(2,1)S(1)}, bf16[64,1280]{1,0:T(8,128)(2,1)S(1)}, u32[]{:S(2)}, u32[]{:S(2)}) collective-permute-start(bf16[64,1280]{1,0:T(8,128)(2,1)S(1)} %get-tuple-element.54), channel_id=1, source_target_pairs={{0,16},{4,20},{8,24},{12,28},{16,0},{20,4},{24,8},{28,12},{1,17},{... | collective-permute-start | bytes 491528 | tf_op jit(solution)/shard_map/ppermute | solution.py:66
  29.0 47.7 %slice-start.5 = ((s8[7864320]{0:T(1024)(128)(4,1)}), s8[3670016]{0:T(1024)(128)(4,1)S(1)}, s32[]{:S(2)}) async-start(s8[7864320]{0:T(1024)(128)(4,1)} %bitcast.13), calls=%async_computation.5 | async-start | bytes 7340032
  29.0 9.5 %collective-permute-start.9 = (bf16[64,1280]{1,0:T(8,128)(2,1)S(1)}, bf16[64,1280]{1,0:T(8,128)(2,1)S(1)}, u32[]{:S(2)}, u32[]{:S(2)}) collective-permute-start(bf16[64,1280]{1,0:T(8,128)(2,1)S(1)} %get-tuple-element.55), channel_id=1, source_target_pairs={{0,24},{4,28},{8,16},{12,20},{16,8},{20,12},{24,0},{28,4},{1,25},{... | collective-permute-start | bytes 491528 | tf_op jit(solution)/shard_map/ppermute | solution.py:66
  34.6 42.1 %slice-start.2 = ((s8[7864320]{0:T(1024)(128)(4,1)}), s8[4194304]{0:T(1024)(128)(4,1)S(1)}, s32[]{:S(2)}) async-start(s8[7864320]{0:T(1024)(128)(4,1)} %bitcast.11), calls=%async_computation.2 | async-start | bytes 8388608
  34.9 10.7 %collective-permute-start.18 = (bf16[4,32,1280]{2,1,0:T(8,128)(2,1)S(1)}, bf16[4,32,1280]{2,1,0:T(8,128)(2,1)S(1)}, u32[]{:S(2)}, u32[]{:S(2)}) collective-permute-start(bf16[4,32,1280]{2,1,0:T(8,128)(2,1)S(1)} %get-tuple-element.59), channel_id=1, source_target_pairs={{0,8},{4,12},{8,0},{12,4},{16,24},{20,28},{24,16},{28,20},{1,9},{5... | collective-permute-start | bytes 983048 | tf_op jit(solution)/shard_map/ppermute | solution.py:66
  36.5 16.4 %collective-permute-start.19 = (bf16[4,32,1280]{2,1,0:T(8,128)(2,1)S(1)}, bf16[4,32,1280]{2,1,0:T(8,128)(2,1)S(1)}, u32[]{:S(2)}, u32[]{:S(2)}) collective-permute-start(bf16[4,32,1280]{2,1,0:T(8,128)(2,1)S(1)} %get-tuple-element.60), channel_id=1, source_target_pairs={{0,16},{4,20},{8,24},{12,28},{16,0},{20,4},{24,8},{28,12},{1,17},{... | collective-permute-start | bytes 983048 | tf_op jit(solution)/shard_map/ppermute | solution.py:66
  38.0 14.9 %collective-permute-start.20 = (bf16[4,32,1280]{2,1,0:T(8,128)(2,1)S(1)}, bf16[4,32,1280]{2,1,0:T(8,128)(2,1)S(1)}, u32[]{:S(2)}, u32[]{:S(2)}) collective-permute-start(bf16[4,32,1280]{2,1,0:T(8,128)(2,1)S(1)} %get-tuple-element.61), channel_id=1, source_target_pairs={{0,24},{4,28},{8,16},{12,20},{16,8},{20,12},{24,0},{28,4},{1,25},{... | collective-permute-start | bytes 983048 | tf_op jit(solution)/shard_map/ppermute | solution.py:66
  38.5 38.2 %slice-start = ((s8[7864320]{0:T(1024)(128)(4,1)}), s8[4194304]{0:T(1024)(128)(4,1)S(1)}, s32[]{:S(2)}) async-start(s8[7864320]{0:T(1024)(128)(4,1)} %bitcast.9), calls=%async_computation | async-start | bytes 8388608
  38.5 38.2 %slice-start.3 = ((s8[7864320]{0:T(1024)(128)(4,1)}), s8[3670016]{0:T(1024)(128)(4,1)S(1)}, s32[]{:S(2)}) async-start(s8[7864320]{0:T(1024)(128)(4,1)} %bitcast.11), calls=%async_computation.3 | async-start | bytes 7340032
  38.5 38.2 %copy-start = (f32[5120]{0:T(1024)S(1)}, f32[5120]{0:T(1024)}, u32[]{:S(2)}) copy-start(f32[5120]{0:T(1024)} %param.12) | copy-start | bytes 61444
  38.7 15.5 %collective-permute-start.11 = (bf16[104,1280]{1,0:T(8,128)(2,1)S(1)}, bf16[104,1280]{1,0:T(8,128)(2,1)S(1)}, u32[]{:S(2)}, u32[]{:S(2)}) collective-permute-start(bf16[104,1280]{1,0:T(8,128)(2,1)S(1)} %get-tuple-element.56.refs_9_), channel_id=1, source_target_pairs={{0,2},{1,3},{2,0},{3,1},{4,6},{5,7},{6,4},{7,5},{8,10},{9,11},{10,... | collective-permute-start | bytes 798728 | tf_op jit(solution)/shard_map/ppermute | solution.py:205
  40.3 13.9 %collective-permute-start.21 = (bf16[4,32,1280]{2,1,0:T(8,128)(2,1)S(1)}, bf16[4,32,1280]{2,1,0:T(8,128)(2,1)S(1)}, u32[]{:S(2)}, u32[]{:S(2)}) collective-permute-start(bf16[4,32,1280]{2,1,0:T(8,128)(2,1)S(1)} %get-tuple-element.58.refs_0_), channel_id=1, source_target_pairs={{0,4},{4,0},{8,12},{12,8},{16,20},{20,16},{24,28},{28,24},{1,5},{5... | collective-permute-start | bytes 983048 | tf_op jit(solution)/shard_map/ppermute | solution.py:72
  45.6 9.4 %collective-permute-start.22 = (bf16[4,32,1280]{2,1,0:T(8,128)(2,1)S(1)}, bf16[4,32,1280]{2,1,0:T(8,128)(2,1)S(1)}, u32[]{:S(2)}, u32[]{:S(2)}) collective-permute-start(bf16[4,32,1280]{2,1,0:T(8,128)(2,1)S(1)} %collective-permute-done.18.refs_1_), channel_id=1, source_target_pairs={{0,4},{4,0},{8,12},{12,8},{16,20},{20,16},{24,28},{28,24},{1,5},{5... | collective-permute-start | bytes 983048 | tf_op jit(solution)/shard_map/ppermute | solution.py:72
  52.9 7.4 %collective-permute-start.23 = (bf16[4,32,1280]{2,1,0:T(8,128)(2,1)S(1)}, bf16[4,32,1280]{2,1,0:T(8,128)(2,1)S(1)}, u32[]{:S(2)}, u32[]{:S(2)}) collective-permute-start(bf16[4,32,1280]{2,1,0:T(8,128)(2,1)S(1)} %collective-permute-done.19.refs_2_), channel_id=1, source_target_pairs={{0,4},{4,0},{8,12},{12,8},{16,20},{20,16},{24,28},{28,24},{1,5},{5... | collective-permute-start | bytes 983048 | tf_op jit(solution)/shard_map/ppermute | solution.py:72
  52.9 8.7 %collective-permute-start.24 = (bf16[4,32,1280]{2,1,0:T(8,128)(2,1)S(1)}, bf16[4,32,1280]{2,1,0:T(8,128)(2,1)S(1)}, u32[]{:S(2)}, u32[]{:S(2)}) collective-permute-start(bf16[4,32,1280]{2,1,0:T(8,128)(2,1)S(1)} %collective-permute-done.20.refs_3_), channel_id=1, source_target_pairs={{0,4},{4,0},{8,12},{12,8},{16,20},{20,16},{24,28},{28,24},{1,5},{5... | collective-permute-start | bytes 983048 | tf_op jit(solution)/shard_map/ppermute | solution.py:72
  54.2 9.1 %collective-permute-start.10 = (bf16[104,1280]{1,0:T(8,128)(2,1)S(1)}, bf16[104,1280]{1,0:T(8,128)(2,1)S(1)}, u32[]{:S(2)}, u32[]{:S(2)}) collective-permute-start(bf16[104,1280]{1,0:T(8,128)(2,1)S(1)} %get-tuple-element.56.refs_9_), channel_id=1, source_target_pairs={{0,1},{1,0},{2,3},{3,2},{4,5},{5,4},{6,7},{7,6},{8,9},{9,8},{10,11... | collective-permute-start | bytes 798728 | tf_op jit(solution)/shard_map/ppermute | solution.py:205
  54.2 10.3 %collective-permute-start.12 = (bf16[104,1280]{1,0:T(8,128)(2,1)S(1)}, bf16[104,1280]{1,0:T(8,128)(2,1)S(1)}, u32[]{:S(2)}, u32[]{:S(2)}) collective-permute-start(bf16[104,1280]{1,0:T(8,128)(2,1)S(1)} %get-tuple-element.56.refs_9_), channel_id=1, source_target_pairs={{1,2},{2,1},{5,6},{6,5},{9,10},{10,9},{13,14},{14,13},{17,18},{18,... | collective-permute-start | bytes 798728 | tf_op jit(solution)/shard_map/ppermute | solution.py:205
  55.0 31.2 %collective-permute-start.29 = (bf16[128,1280]{1,0:T(8,128)(2,1)S(1)}, bf16[128,1280]{1,0:T(8,128)(2,1)S(1)}, u32[]{:S(2)}, u32[]{:S(2)}) collective-permute-start(bf16[128,1280]{1,0:T(8,128)(2,1)S(1)} %get-tuple-element.71.refs_9_), channel_id=1, source_target_pairs={{0,2},{1,3},{2,0},{3,1},{4,6},{5,7},{6,4},{7,5},{8,10},{9,11},{10,... | collective-permute-start | bytes 983048 | tf_op jit(solution)/shard_map/ppermute | solution.py:205
  60.3 9.6 %collective-permute-start.13 = (bf16[104,1280]{1,0:T(8,128)(2,1)S(1)}, bf16[104,1280]{1,0:T(8,128)(2,1)S(1)}, u32[]{:S(2)}, u32[]{:S(2)}) collective-permute-start(bf16[104,1280]{1,0:T(8,128)(2,1)S(1)} %collective-permute-done.11.refs_11_), channel_id=1, source_target_pairs={{1,0},{2,3},{5,4},{6,7},{9,8},{10,11},{13,12},{14,15},{17,16},{18,... | collective-permute-start | bytes 798728 | tf_op jit(solution)/shard_map/ppermute | solution.py:205
  62.4 24.5 %collective-permute-start.25 = (bf16[4,32,1280]{2,1,0:T(8,128)(2,1)S(1)}, bf16[4,32,1280]{2,1,0:T(8,128)(2,1)S(1)}, u32[]{:S(2)}, u32[]{:S(2)}) collective-permute-start(bf16[4,32,1280]{2,1,0:T(8,128)(2,1)S(1)} %get-tuple-element.63), channel_id=1, source_target_pairs={{0,8},{4,12},{8,0},{12,4},{16,24},{20,28},{24,16},{28,20},{1,9},{5... | collective-permute-start | bytes 983048 | tf_op jit(solution)/shard_map/ppermute | solution.py:66
  63.2 25.2 %collective-permute-start.26 = (bf16[4,32,1280]{2,1,0:T(8,128)(2,1)S(1)}, bf16[4,32,1280]{2,1,0:T(8,128)(2,1)S(1)}, u32[]{:S(2)}, u32[]{:S(2)}) collective-permute-start(bf16[4,32,1280]{2,1,0:T(8,128)(2,1)S(1)} %get-tuple-element.64), channel_id=1, source_target_pairs={{0,16},{4,20},{8,24},{12,28},{16,0},{20,4},{24,8},{28,12},{1,17},{... | collective-permute-start | bytes 983048 | tf_op jit(solution)/shard_map/ppermute | solution.py:66
  64.5 23.9 %collective-permute-start.27 = (bf16[4,32,1280]{2,1,0:T(8,128)(2,1)S(1)}, bf16[4,32,1280]{2,1,0:T(8,128)(2,1)S(1)}, u32[]{:S(2)}, u32[]{:S(2)}) collective-permute-start(bf16[4,32,1280]{2,1,0:T(8,128)(2,1)S(1)} %get-tuple-element.65), channel_id=1, source_target_pairs={{0,24},{4,28},{8,16},{12,20},{16,8},{20,12},{24,0},{28,4},{1,25},{... | collective-permute-start | bytes 983048 | tf_op jit(solution)/shard_map/ppermute | solution.py:66
  69.9 25.6 %collective-permute-start.28 = (bf16[128,1280]{1,0:T(8,128)(2,1)S(1)}, bf16[128,1280]{1,0:T(8,128)(2,1)S(1)}, u32[]{:S(2)}, u32[]{:S(2)}) collective-permute-start(bf16[128,1280]{1,0:T(8,128)(2,1)S(1)} %get-tuple-element.71.refs_9_), channel_id=1, source_target_pairs={{0,1},{1,0},{2,3},{3,2},{4,5},{5,4},{6,7},{7,6},{8,9},{9,8},{10,11... | collective-permute-start | bytes 983048 | tf_op jit(solution)/shard_map/ppermute | solution.py:205
  86.2 9.3 %collective-permute-start.30 = (bf16[128,1280]{1,0:T(8,128)(2,1)S(1)}, bf16[128,1280]{1,0:T(8,128)(2,1)S(1)}, u32[]{:S(2)}, u32[]{:S(2)}) collective-permute-start(bf16[128,1280]{1,0:T(8,128)(2,1)S(1)} %get-tuple-element.71.refs_9_), channel_id=1, source_target_pairs={{1,2},{2,1},{5,6},{6,5},{9,10},{10,9},{13,14},{14,13},{17,18},{18,... | collective-permute-start | bytes 983048 | tf_op jit(solution)/shard_map/ppermute | solution.py:205
  86.9 9.6 %collective-permute-start.31 = (bf16[128,1280]{1,0:T(8,128)(2,1)S(1)}, bf16[128,1280]{1,0:T(8,128)(2,1)S(1)}, u32[]{:S(2)}, u32[]{:S(2)}) collective-permute-start(bf16[128,1280]{1,0:T(8,128)(2,1)S(1)} %collective-permute-done.29.refs_11_), channel_id=1, source_target_pairs={{1,0},{2,3},{5,4},{6,7},{9,8},{10,11},{13,12},{14,15},{17,16},{18,... | collective-permute-start | bytes 983048 | tf_op jit(solution)/shard_map/ppermute | solution.py:205
  111.8 9.7 %collective-permute-start.34 = (bf16[104,1280]{1,0:T(8,128)(2,1)S(1)}, bf16[104,1280]{1,0:T(8,128)(2,1)S(1)}, u32[]{:S(2)}, u32[]{:S(2)}) collective-permute-start(bf16[104,1280]{1,0:T(8,128)(2,1)S(1)} %shard_map.125), channel_id=1, source_target_pairs={{0,1},{1,0},{2,3},{3,2},{4,5},{5,4},{6,7},{7,6},{8,9},{9,8},{10,11... | collective-permute-start | bytes 798728 | tf_op jit(solution)/shard_map/ppermute | solution.py:541
  114.1 20.1 %collective-permute-start.33 = (bf16[104,1280]{1,0:T(8,128)(2,1)S(1)}, bf16[104,1280]{1,0:T(8,128)(2,1)S(1)}, u32[]{:S(2)}, u32[]{:S(2)}) collective-permute-start(bf16[104,1280]{1,0:T(8,128)(2,1)S(1)} %shard_map.124), channel_id=1, source_target_pairs={{0,2},{1,3},{2,0},{3,1},{4,6},{5,7},{6,4},{7,5},{8,10},{9,11},{10,... | collective-permute-start | bytes 798728 | tf_op jit(solution)/shard_map/ppermute | solution.py:541
  115.0 19.2 %collective-permute-start.32 = (bf16[104,1280]{1,0:T(8,128)(2,1)S(1)}, bf16[104,1280]{1,0:T(8,128)(2,1)S(1)}, u32[]{:S(2)}, u32[]{:S(2)}) collective-permute-start(bf16[104,1280]{1,0:T(8,128)(2,1)S(1)} %shard_map.123), channel_id=1, source_target_pairs={{0,3},{1,2},{2,1},{3,0},{4,7},{5,6},{6,5},{7,4},{8,11},{9,10},{10,... | collective-permute-start | bytes 798728 | tf_op jit(solution)/shard_map/ppermute | solution.py:541
  134.5 4.5 %collective-permute-start.35 = (bf16[32,1280]{1,0:T(8,128)(2,1)S(1)}, bf16[32,1280]{1,0:T(8,128)(2,1)S(1)}, u32[]{:S(2)}, u32[]{:S(2)}) collective-permute-start(bf16[32,1280]{1,0:T(8,128)(2,1)S(1)} %get-tuple-element.85), channel_id=1, source_target_pairs={{0,8},{4,12},{8,0},{12,4},{16,24},{20,28},{24,16},{28,20},{1,9},{5... | collective-permute-start | bytes 245768 | tf_op jit(solution)/shard_map/ppermute | solution.py:66
  136.0 4.4 %collective-permute-start.36 = (bf16[32,1280]{1,0:T(8,128)(2,1)S(1)}, bf16[32,1280]{1,0:T(8,128)(2,1)S(1)}, u32[]{:S(2)}, u32[]{:S(2)}) collective-permute-start(bf16[32,1280]{1,0:T(8,128)(2,1)S(1)} %get-tuple-element.86), channel_id=1, source_target_pairs={{0,16},{4,20},{8,24},{12,28},{16,0},{20,4},{24,8},{28,12},{1,17},{... | collective-permute-start | bytes 245768 | tf_op jit(solution)/shard_map/ppermute | solution.py:66
  136.5 5.3 %collective-permute-start.37 = (bf16[32,1280]{1,0:T(8,128)(2,1)S(1)}, bf16[32,1280]{1,0:T(8,128)(2,1)S(1)}, u32[]{:S(2)}, u32[]{:S(2)}) collective-permute-start(bf16[32,1280]{1,0:T(8,128)(2,1)S(1)} %get-tuple-element.87), channel_id=1, source_target_pairs={{0,24},{4,28},{8,16},{12,20},{16,8},{20,12},{24,0},{28,4},{1,25},{... | collective-permute-start | bytes 245768 | tf_op jit(solution)/shard_map/ppermute | solution.py:66
  143.0 1.7 %collective-permute-start.38 = (bf16[4,32,1280]{2,1,0:T(8,128)(2,1)S(1)}, bf16[4,32,1280]{2,1,0:T(8,128)(2,1)S(1)}, u32[]{:S(2)}, u32[]{:S(2)}) collective-permute-start(bf16[4,32,1280]{2,1,0:T(8,128)(2,1)S(1)} %get-tuple-element.89), channel_id=1, source_target_pairs={{0,4},{4,0},{8,12},{12,8},{16,20},{20,16},{24,28},{28,24},{1,5},{5... | collective-permute-start | bytes 983048 | tf_op jit(solution)/shard_map/ppermute | solution.py:72
  144.7 4.6 %collective-permute-start.39 = (bf16[32,1280]{1,0:T(8,128)(2,1)S(1)}, bf16[32,1280]{1,0:T(8,128)(2,1)S(1)}, u32[]{:S(2)}, u32[]{:S(2)}) collective-permute-start(bf16[32,1280]{1,0:T(8,128)(2,1)S(1)} %get-tuple-element.91), channel_id=1, source_target_pairs={{0,8},{4,12},{8,0},{12,4},{16,24},{20,28},{24,16},{28,20},{1,9},{5... | collective-permute-start | bytes 245768 | tf_op jit(solution)/shard_map/ppermute | solution.py:66
  146.4 6.2 %collective-permute-start.40 = (bf16[32,1280]{1,0:T(8,128)(2,1)S(1)}, bf16[32,1280]{1,0:T(8,128)(2,1)S(1)}, u32[]{:S(2)}, u32[]{:S(2)}) collective-permute-start(bf16[32,1280]{1,0:T(8,128)(2,1)S(1)} %get-tuple-element.92), channel_id=1, source_target_pairs={{0,16},{4,20},{8,24},{12,28},{16,0},{20,4},{24,8},{28,12},{1,17},{... | collective-permute-start | bytes 245768 | tf_op jit(solution)/shard_map/ppermute | solution.py:66
  146.9 5.7 %collective-permute-start.41 = (bf16[32,1280]{1,0:T(8,128)(2,1)S(1)}, bf16[32,1280]{1,0:T(8,128)(2,1)S(1)}, u32[]{:S(2)}, u32[]{:S(2)}) collective-permute-start(bf16[32,1280]{1,0:T(8,128)(2,1)S(1)} %get-tuple-element.93), channel_id=1, source_target_pairs={{0,24},{4,28},{8,16},{12,20},{16,8},{20,12},{24,0},{28,4},{1,25},{... | collective-permute-start | bytes 245768 | tf_op jit(solution)/shard_map/ppermute | solution.py:66
  (7 other events, 128.1 us)
